TPU v7x, 256 devices: a whole 4x4x8 slice. The times are simulated.
256 devices in a mesh: cells: 16 (over y, z_hi), grp: 16 (over x, z_lo, core).
Axes of the slice: x: 4, y: 4, z: 8 (z_hi: 4, z_lo: 2; z = z_hi * 2 + z_lo), core: 2. Of those that a mesh axis runs over, the one named last changes fastest.
Arguments:
- coeffs: bfloat16 [4096, 6144], P(('cells', 'grp')), may hold values from -6 to 6
- neighbours: int32 [4096, 32], P(('cells', 'grp')), may hold values from 0 to 47
- counts: int32 [4096], P(('cells', 'grp')), may hold values from 8 to 32
- boxes: int32 [4096], P(('cells', 'grp')), may hold values from 0 to 31
- axial: bfloat16 [4096, 32, 96], P(('cells', 'grp')), may hold values from -1 to 1
- rotations: bfloat16 [32, 96, 96], replicated, may hold values from -0.625 to 0.625
- out_map: bfloat16 [96, 96], replicated, may hold values from -0.625 to 0.625
- coupling: bfloat16 [512, 512], replicated, may hold values from -1 to 1, as said below
- in_map: bfloat16 [96, 96], replicated, may hold values from -0.21875 to 0.21875
- tmat: float32 [4096, 96], P(('cells', 'grp')), may hold values from -0.5 to 0.5
Outputs:
- product: bfloat16 [4096, 6144], P(('cells', 'grp'))
Inputs may be any that keep to these rules, and one draw needn't show every extreme that they name: Entries of coupling are zero on the diagonal.
All inputs are finite; a program needn't handle non-finite values.
Results may differ from a plain program's by a relative error of at most 0.0043.
Values may be sent and summed in bfloat16 or wider, within the bound.
No kernel may reach another device: no remote copies, remote signals or barrier semaphores. Data moves between devices by JAX's collectives and lax.ppermute only.
A program may use at most 64 MiB of HBM per device.

v0:
```python
import jax
import jax.numpy as jnp
from jax import lax
from jax.sharding import PartitionSpec as P

NBG = 2


slot_width = 8


def padded(block, sides, width):
    for axis, dim in sides:
        count = lax.axis_size(axis)
        forward = [(i, i + 1) for i in range(count - 1)]
        backward = [(target, source) for source, target in forward]
        low = lax.ppermute(
            lax.slice_in_dim(block, block.shape[dim] - width, None, axis=dim), axis, forward
        )
        high = lax.ppermute(lax.slice_in_dim(block, 0, width, axis=dim), axis, backward)
        block = jnp.concatenate([low, block, high], axis=dim)
    return block


def in_blocks(value, dim, size):
    dims = value.shape
    blocks = value.reshape(*dims[:dim], size, dims[dim] // size, *dims[dim + 1 :])
    return jnp.moveaxis(blocks, dim, 0)


def summed_on_arrival(value, axis, dim):
    blocks = in_blocks(value, dim, lax.axis_size(axis))
    arrived = lax.all_to_all(blocks, axis, split_axis=0, concat_axis=0, tiled=True)
    return arrived.sum(axis=0)


def laid_out(blocks, dim):
    blocks = jnp.moveaxis(blocks, 0, dim)
    dims = blocks.shape
    return blocks.reshape(*dims[:dim], dims[dim] * dims[dim + 1], *dims[dim + 2 :])


def sent_to_all(value, axis):
    size = lax.axis_size(axis)
    return lax.all_to_all(
        jnp.broadcast_to(value[None], (size, *value.shape)), axis, 0, 0, tiled=True
    )


def collect(value, axis, dim):
    return laid_out(sent_to_all(value, axis), dim)


def near_field(cand, nbr, cnt, axial, rot):
    sd, slots = nbr.shape
    width = rot.shape[1]
    incid = cand.shape[1] // width
    groups = slots // slot_width
    live = (lax.broadcasted_iota(jnp.int32, (sd, slots), 1) < cnt[:, None]).astype(jnp.float32)
    scale = axial.astype(jnp.float32) * live[:, :, None]
    idx_groups = nbr.reshape(sd, groups, slot_width).transpose(1, 0, 2)
    scale_groups = scale.reshape(sd, groups, slot_width, width).transpose(1, 0, 2, 3)
    rot_groups = rot.reshape(groups, slot_width, width, width)

    def step(total, item):
        idx, factor, rg = item
        picked = cand[idx].reshape(sd, slot_width, width, incid)
        turned = jnp.einsum("kdc,skcp->skdp", rg, picked, preferred_element_type=jnp.float32)
        scaled = (turned * factor[..., None]).astype(jnp.bfloat16)
        back = jnp.einsum("kdc,skdp->scp", rg, scaled, preferred_element_type=jnp.float32)
        return (total + back, None)

    start = jnp.zeros((sd, width, incid), jnp.float32)
    total, _ = lax.scan(step, start, (idx_groups, scale_groups, rot_groups))
    return total


def apply_tmat(field, tmat):
    half = field.shape[1] // 2
    real_t = tmat[:, :half, None]
    imag_t = tmat[:, half:, None]
    real_u = field[:, :half]
    imag_u = field[:, half:]
    return jnp.concatenate(
        [real_t * real_u - imag_t * imag_u, real_t * imag_u + imag_t * real_u], axis=1
    )


def shards(coeffs, neighbours, counts, boxes, axial, rotations, out_map, coupling, in_map, tmat):
    sd = coeffs.shape[0]
    width = rotations.shape[1]
    incid = coeffs.shape[1] // width
    ngrp = lax.axis_size("grp")
    ncell = lax.axis_size("cells")
    nbc = NBG * ngrp
    column = lax.axis_index("cells")
    cand = padded(coeffs, (("cells", 0),), sd)
    near = near_field(cand, neighbours, counts, axial, rotations)
    onehot = (boxes[:, None] == lax.broadcasted_iota(jnp.int32, (sd, nbc), 1)).astype(jnp.bfloat16)
    partial_sums = lax.dot_general(
        onehot, coeffs, (((0,), (0,)), ((), ())), preferred_element_type=jnp.float32
    )
    summed = summed_on_arrival(partial_sums, "grp", 0)
    summed = summed.reshape(NBG, width, incid)
    moments = jnp.einsum(
        "dc,bcp->bdp", out_map.astype(jnp.float32), summed, precision=lax.Precision.HIGHEST
    )
    moments = moments.astype(jnp.bfloat16).reshape(NBG, width * incid)
    rows = lax.dynamic_slice_in_dim(coupling, column * nbc, nbc, 0)
    rows = rows.reshape(nbc, ncell, ngrp, NBG)
    picked_cols = lax.dynamic_slice_in_dim(rows, lax.axis_index("grp"), 1, 2).reshape(
        nbc, ncell * NBG
    )
    partial_local = jnp.dot(
        picked_cols, collect(moments, "cells", 0), preferred_element_type=jnp.float32
    )
    local = lax.psum(partial_local, "grp").astype(jnp.bfloat16)
    chosen = jnp.dot(onehot, local, preferred_element_type=jnp.float32).astype(jnp.bfloat16)
    chosen = chosen.reshape(sd, width, incid)
    far = jnp.einsum("dc,scp->sdp", in_map, chosen, preferred_element_type=jnp.float32)
    field = near + far
    turned = apply_tmat(field, tmat).reshape(sd, width * incid)
    return (coeffs.astype(jnp.float32) - turned).astype(jnp.bfloat16)


def solution(mesh):
    in_specs = (
        P(("cells", "grp"), None),
        P(("cells", "grp"), None),
        P(("cells", "grp")),
        P(("cells", "grp")),
        P(("cells", "grp"), None, None),
        P(),
        P(),
        P(),
        P(),
        P(("cells", "grp"), None),
    )
    out_specs = P(("cells", "grp"), None)
    return jax.shard_map(shards, mesh=mesh, in_specs=in_specs, out_specs=out_specs, check_vma=False)
```

profile of v0, /device:TPU:8, one launch (start us, length us, event | category | flops | bytes accessed | tf_op | source)
XLA Modules:
  0.0 151.2 jit_solution(943825938569145490)
XLA Ops:
  0.0 8.2 %collective-permute-start.1 = (bf16[16,6144]{1,0:T(8,128)(2,1)}, bf16[16,6144]{1,0:T(8,128)(2,1)S(1)}, u32[]{:S(2)}, u32[]{:S(2)}) collective-permute-start(bf16[16,6144]{1,0:T(8,128)(2,1)} %param.12), channel_id=1, source_target_pairs={{16,0},{32,16},{48,32},{64,48},{80,64},{96,80},{112,96},{128,112},... | collective-permute-start | bytes 589832 | tf_op jit(solution)/shard_map/ppermute | solution.py:20
  8.3 1.9 %collective-permute-start = (bf16[16,6144]{1,0:T(8,128)(2,1)}, bf16[16,6144]{1,0:T(8,128)(2,1)S(1)}, u32[]{:S(2)}, u32[]{:S(2)}) collective-permute-start(bf16[16,6144]{1,0:T(8,128)(2,1)} %param.12), channel_id=1, source_target_pairs={{0,16},{16,32},{32,48},{48,64},{64,80},{80,96},{96,112},{112,128},... | collective-permute-start | bytes 589832 | tf_op jit(solution)/shard_map/ppermute | solution.py:17
  10.2 1.3 fusion.14
  11.6 1.4 reshape.92
  12.9 5.0 %all-to-all-start = ((f32[16,2,6144]{2,1,0:T(2,128)}), f32[16,2,6144]{2,1,0:T(2,128)S(1)}, u32[]{:S(2)}, u32[]{:S(2)}) async-start(f32[16,2,6144]{2,1,0:T(2,128)} %reshape.92), calls=%async_computation | async-start | bytes 1572864 | tf_op jit(solution)/shard_map/all_to_all | solution.py:33
  18.0 0.1 copy.26
  18.3 0.1 multiply_bitcast_fusion
  18.4 0.7 fusion.18
  19.1 4.2 %collective-permute-done = bf16[16,6144]{1,0:T(8,128)(2,1)S(1)} collective-permute-done((bf16[16,6144]{1,0:T(8,128)(2,1)}, bf16[16,6144]{1,0:T(8,128)(2,1)S(1)}, u32[]{:S(2)}, u32[]{:S(2)}) %collective-permute-start) | collective-permute-done | bytes 196640 | tf_op jit(solution)/shard_map/ppermute | solution.py:17
  23.4 8.3 %all-to-all-done = f32[16,2,6144]{2,1,0:T(2,128)S(1)} async-done(((f32[16,2,6144]{2,1,0:T(2,128)}), f32[16,2,6144]{2,1,0:T(2,128)S(1)}, u32[]{:S(2)}, u32[]{:S(2)}) %all-to-all-start) | async-done | bytes 786464 | tf_op jit(solution)/shard_map/all_to_all | solution.py:33
  31.6 0.3 reduce_sum.9
  31.9 0.1 reshape.93
  32.0 0.2 fusion.10
  32.3 0.1 copy.19
  32.4 0.1 broadcast_in_dim.9
  32.5 1.0 broadcast_in_dim.10
  33.5 9.5 %all-to-all-start.1 = ((bf16[16,2,6144]{2,1,0:T(2,128)(2,1)}), bf16[16,2,6144]{2,1,0:T(2,128)(2,1)S(1)}, u32[]{:S(2)}, u32[]{:S(2)}) async-start(bf16[16,2,6144]{2,1,0:T(2,128)(2,1)} %broadcast_in_dim.10), calls=%async_computation.1 | async-start | bytes 786432 | tf_op jit(solution)/shard_map/all_to_all | solution.py:45
  43.0 43.2 %while.11 = (s32[]{:T(128)}, f32[16,96,64]{1,2,0:T(8,128)}, s32[4,16,8]{1,2,0:T(8,128)S(1)}, bf16[48,6144]{1,0:T(8,128)(2,1)S(1)}, bf16[4,8,96,96]{3,2,1,0:T(8,1...) while((s32[]{:T(128)}, f32[16,96,64]{1,2,0:T(8,128)}, ...), condition=%wide.region_1.2_spmd.clone, body=%wide.region_0.1_spmd.clone.sunk | while | flops 303760768 | bytes 10921638 | solution.py:74
  43.1 0.1 reshape.121
  43.2 0.4 copy-done.4
  43.6 1.5 gather_fusion
  45.1 4.2 %reshape.122 = bf16[16,8,96,64]{3,2,1,0:T(8,128)(2,1)} reshape(bf16[128,6144]{1,0:T(8,128)(2,1)S(1)} %gather_fusion) | data formatting | bytes 3145728 | tf_op jit(solution)/shard_map/while/body/eval_jaxpr/reshape | solution.py:67
  49.3 4.3 %fusion.34 = f32[16,96,64]{1,2,0:T(8,128)} fusion(bf16[16,8,96,64]{3,2,1,0:T(8,128)(2,1)} %reshape.122, f32[16,8,96]{2,1,0:T(8,128)S(1)} %dynamic-slice_bitcast_fusion.2, f32[16,96,64]{1,2,0:T(8,128)} %get-tuple-element.127, pred[]{:T(512)S(6)} %compare.3, bf16[4,8,96,96]{3,2,1,0:T(8,128)(2,1)} %get-tuple-element.138, s32[]{:T(128)S(6)} %copy.31), kind=kOutput, calls=%fused_computation.5.clone.1 | convolution fusion | flops 303759360 | bytes 4507136 | tf_op jit(solution)/shard_map/while/body/eval_jaxpr/kdc,skdp->scp/dot_general | solution.py:70
  53.7 0.1 reshape.121
  53.8 0.4 copy-done.4
  54.3 1.5 gather_fusion
  55.8 4.2 %reshape.122 = bf16[16,8,96,64]{3,2,1,0:T(8,128)(2,1)} reshape(bf16[128,6144]{1,0:T(8,128)(2,1)S(1)} %gather_fusion) | data formatting | bytes 3145728 | tf_op jit(solution)/shard_map/while/body/eval_jaxpr/reshape | solution.py:67
  60.0 4.5 %fusion.34 = f32[16,96,64]{1,2,0:T(8,128)} fusion(bf16[16,8,96,64]{3,2,1,0:T(8,128)(2,1)} %reshape.122, f32[16,8,96]{2,1,0:T(8,128)S(1)} %dynamic-slice_bitcast_fusion.2, f32[16,96,64]{1,2,0:T(8,128)} %get-tuple-element.127, pred[]{:T(512)S(6)} %compare.3, bf16[4,8,96,96]{3,2,1,0:T(8,128)(2,1)} %get-tuple-element.138, s32[]{:T(128)S(6)} %copy.31), kind=kOutput, calls=%fused_computation.5.clone.1 | convolution fusion | flops 303759360 | bytes 4507136 | tf_op jit(solution)/shard_map/while/body/eval_jaxpr/kdc,skdp->scp/dot_general | solution.py:70
  64.6 0.1 reshape.121
  64.7 0.4 copy-done.4
  65.1 1.5 gather_fusion
  66.6 4.2 %reshape.122 = bf16[16,8,96,64]{3,2,1,0:T(8,128)(2,1)} reshape(bf16[128,6144]{1,0:T(8,128)(2,1)S(1)} %gather_fusion) | data formatting | bytes 3145728 | tf_op jit(solution)/shard_map/while/body/eval_jaxpr/reshape | solution.py:67
  70.9 4.5 %fusion.34 = f32[16,96,64]{1,2,0:T(8,128)} fusion(bf16[16,8,96,64]{3,2,1,0:T(8,128)(2,1)} %reshape.122, f32[16,8,96]{2,1,0:T(8,128)S(1)} %dynamic-slice_bitcast_fusion.2, f32[16,96,64]{1,2,0:T(8,128)} %get-tuple-element.127, pred[]{:T(512)S(6)} %compare.3, bf16[4,8,96,96]{3,2,1,0:T(8,128)(2,1)} %get-tuple-element.138, s32[]{:T(128)S(6)} %copy.31), kind=kOutput, calls=%fused_computation.5.clone.1 | convolution fusion | flops 303759360 | bytes 4507136 | tf_op jit(solution)/shard_map/while/body/eval_jaxpr/kdc,skdp->scp/dot_general | solution.py:70
  75.5 0.4 copy-done.4
  76.0 1.5 gather_fusion
  77.5 4.2 %reshape.122 = bf16[16,8,96,64]{3,2,1,0:T(8,128)(2,1)} reshape(bf16[128,6144]{1,0:T(8,128)(2,1)S(1)} %gather_fusion) | data formatting | bytes 3145728 | tf_op jit(solution)/shard_map/while/body/eval_jaxpr/reshape | solution.py:67
  81.7 4.5 %fusion.34 = f32[16,96,64]{1,2,0:T(8,128)} fusion(bf16[16,8,96,64]{3,2,1,0:T(8,128)(2,1)} %reshape.122, f32[16,8,96]{2,1,0:T(8,128)S(1)} %dynamic-slice_bitcast_fusion.2, f32[16,96,64]{1,2,0:T(8,128)} %get-tuple-element.127, pred[]{:T(512)S(6)} %compare.3, bf16[4,8,96,96]{3,2,1,0:T(8,128)(2,1)} %get-tuple-element.138, s32[]{:T(128)S(6)} %copy.31), kind=kOutput, calls=%fused_computation.5.clone.1 | convolution fusion | flops 303759360 | bytes 4507136 | tf_op jit(solution)/shard_map/while/body/eval_jaxpr/kdc,skdp->scp/dot_general | solution.py:70
  86.2 0.1 reshape.94
  86.4 0.3 fusion.19
  86.7 61.8 %all-reduce.1 = bf16[32,6144]{1,0:T(8,128)(2,1)S(1)} all-reduce(f32[32,6144]{1,0:T(8,128)S(1)} %fusion.19), channel_id=1, replica_groups=mesh['cells'=16,'grp'=16] {'grp'}, use_global_device_ids=true, to_apply=%region_3.4 | all-reduce | flops 196608 | bytes 1179648 | tf_op jit(solution)/shard_map/psum | solution.py:117
  148.5 0.3 convolution_convert_fusion
  148.7 0.4 reshape.95
  149.1 0.3 convolution_bitcast_fusion
  149.5 0.2 multiply_subtract_fusion
  149.7 0.2 pad_maximum_fusion.1
  150.0 0.3 copy.21
  150.2 0.3 reshape.96
  150.5 0.7 subtract_convert_fusion
  (62 shorter events, 0.8 us)
Async XLA Ops:
  0.0 18.0 %copy-start = (bf16[512,512]{1,0:T(8,128)(2,1)S(1)}, bf16[512,512]{1,0:T(8,128)(2,1)}, u32[]{:S(2)}) copy-start(bf16[512,512]{1,0:T(8,128)(2,1)} %param.19) | copy-start | bytes 1572868
  0.0 17.9 %copy-start.11 = (s32[16,32]{1,0:T(8,128)S(1)}, s32[16,32]{1,0:T(8,128)}, u32[]{:S(2)}) copy-start(s32[16,32]{1,0:T(8,128)} %param.13) | copy-start | bytes 6148
  0.0 18.2 %copy-start.13 = (s32[16]{0:T(128)S(1)}, s32[16]{0:T(128)}, u32[]{:S(2)}) copy-start(s32[16]{0:T(128)} %param.14) | copy-start | bytes 196
  0.0 18.3 %copy-start.3 = (bf16[16,32,96]{2,1,0:T(8,128)(2,1)S(1)}, bf16[16,32,96]{2,1,0:T(8,128)(2,1)}, u32[]{:S(2)}) copy-start(bf16[16,32,96]{2,1,0:T(8,128)(2,1)} %param.16) | copy-start | bytes 294916
  0.0 19.1 %collective-permute-start.1 = (bf16[16,6144]{1,0:T(8,128)(2,1)}, bf16[16,6144]{1,0:T(8,128)(2,1)S(1)}, u32[]{:S(2)}, u32[]{:S(2)}) collective-permute-start(bf16[16,6144]{1,0:T(8,128)(2,1)} %param.12), channel_id=1, source_target_pairs={{16,0},{32,16},{48,32},{64,48},{80,64},{96,80},{112,96},{128,112},... | collective-permute-start | bytes 589832 | tf_op jit(solution)/shard_map/ppermute | solution.py:20
  8.3 15.1 %collective-permute-start = (bf16[16,6144]{1,0:T(8,128)(2,1)}, bf16[16,6144]{1,0:T(8,128)(2,1)S(1)}, u32[]{:S(2)}, u32[]{:S(2)}) collective-permute-start(bf16[16,6144]{1,0:T(8,128)(2,1)} %param.12), channel_id=1, source_target_pairs={{0,16},{16,32},{32,48},{48,64},{64,80},{80,96},{96,112},{112,128},... | collective-permute-start | bytes 589832 | tf_op jit(solution)/shard_map/ppermute | solution.py:17
  11.5 6.9 %copy-start.8 = (f32[16,96]{1,0:T(8,128)S(1)}, f32[16,96]{1,0:T(8,128)}, u32[]{:S(2)}) copy-start(f32[16,96]{1,0:T(8,128)} %param.21) | copy-start | bytes 18436
  11.6 11.8 %copy-start.1 = (bf16[16,6144]{1,0:T(8,128)(2,1)S(1)}, bf16[16,6144]{1,0:T(8,128)(2,1)}, u32[]{:S(2)}) copy-start(bf16[16,6144]{1,0:T(8,128)(2,1)} %param.12) | copy-start | bytes 589828
  12.9 19.1 %copy-start.9 = (bf16[96,96]{1,0:T(8,128)(2,1)S(1)}, bf16[96,96]{1,0:T(8,128)(2,1)}, u32[]{:S(2)}) copy-start(bf16[96,96]{1,0:T(8,128)(2,1)} %param.18) | copy-start | bytes 55300
  12.9 18.7 %all-to-all-start = ((f32[16,2,6144]{2,1,0:T(2,128)}), f32[16,2,6144]{2,1,0:T(2,128)S(1)}, u32[]{:S(2)}, u32[]{:S(2)}) async-start(f32[16,2,6144]{2,1,0:T(2,128)} %reshape.92), calls=%async_computation | async-start | bytes 1572864 | tf_op jit(solution)/shard_map/all_to_all | solution.py:33
  33.5 52.7 %all-to-all-start.1 = ((bf16[16,2,6144]{2,1,0:T(2,128)(2,1)}), bf16[16,2,6144]{2,1,0:T(2,128)(2,1)S(1)}, u32[]{:S(2)}, u32[]{:S(2)}) async-start(bf16[16,2,6144]{2,1,0:T(2,128)(2,1)} %broadcast_in_dim.10), calls=%async_computation.1 | async-start | bytes 786432 | tf_op jit(solution)/shard_map/all_to_all | solution.py:45
  43.0 0.6 copy-start.4
  49.3 4.3 %copy-start.5 = (s32[4,16,8]{1,2,0:T(8,128)S(1)}, s32[4,16,8]{1,2,0:T(8,128)}, u32[]{:S(2)}) copy-start(s32[4,16,8]{1,2,0:T(8,128)} %copy-done.4) | copy-start | bytes 6148 | tf_op jit(solution)/shard_map/while
  53.7 0.6 copy-start.4
  60.0 4.5 %copy-start.5 = (s32[4,16,8]{1,2,0:T(8,128)S(1)}, s32[4,16,8]{1,2,0:T(8,128)}, u32[]{:S(2)}) copy-start(s32[4,16,8]{1,2,0:T(8,128)} %copy-done.4) | copy-start | bytes 6148 | tf_op jit(solution)/shard_map/while
  64.5 0.6 copy-start.4
  70.9 4.5 %copy-start.5 = (s32[4,16,8]{1,2,0:T(8,128)S(1)}, s32[4,16,8]{1,2,0:T(8,128)}, u32[]{:S(2)}) copy-start(s32[4,16,8]{1,2,0:T(8,128)} %copy-done.4) | copy-start | bytes 6148 | tf_op jit(solution)/shard_map/while
  75.3 0.6 copy-start.4
  81.7 4.5 %copy-start.5 = (s32[4,16,8]{1,2,0:T(8,128)S(1)}, s32[4,16,8]{1,2,0:T(8,128)}, u32[]{:S(2)}) copy-start(s32[4,16,8]{1,2,0:T(8,128)} %copy-done.4) | copy-start | bytes 6148 | tf_op jit(solution)/shard_map/while
  86.2 62.3 %copy-start.12 = (s32[16]{0:T(128)S(1)}, s32[16]{0:T(128)}, u32[]{:S(2)}) copy-start(s32[16]{0:T(128)} %param.15) | copy-start | bytes 196
  86.2 62.9 %copy-start.10 = (bf16[96,96]{1,0:T(8,128)(2,1)S(1)}, bf16[96,96]{1,0:T(8,128)(2,1)}, u32[]{:S(2)}) copy-start(bf16[96,96]{1,0:T(8,128)(2,1)} %param.20) | copy-start | bytes 55300
  86.4 63.0 %copy-start.2 = (f32[16,96,64]{1,2,0:T(8,128)S(1)}, f32[16,96,64]{1,2,0:T(8,128)}, u32[]{:S(2)}) copy-start(f32[16,96,64]{1,2,0:T(8,128)} %get-tuple-element.37) | copy-start | bytes 1179652
  148.5 1.0 copy-start.6
  148.5 1.0 copy-start.7
where the time goes:
time: 152 us; the launch traced here: 151 us
  blocking collectives  61.8 us (41%)
  local copies, waits for them, and re-layouts  30 us (20%)
  starting transfers between devices  24.6 us (16%)
  matrix products  20.1 us (13%)
  waiting for transfers between devices  12.5 us (8%)
  other arithmetic  1.76 us (1%)
    psum x1, blocking collectives, shards(): local = lax.psum(partial_local, 'grp').astype(jnp.bfloat16)  61.8 us
    dot_general x4, matrix products, step(): jnp.einsum('kdc,skdp->scp', rg, scaled, preferred_element_type=jnp.float32)  17.7 us
    reshape x4, local copies, waits for them, and re-layouts, step(): picked = cand[idx].reshape(sd, slot_width, width, incid)  16.9 us
    all_to_all x1, starting transfers between devices, sent_to_all(): lax.all_to_all(jnp.broadcast_to(value[None], (size, *value.shape)), axis,...  9.51 us
    all_to_all x1, waiting for transfers between devices, summed_on_arrival(): lax.all_to_all(blocks, axis, split_axis=0, concat_axis=0, tiled=True)  8.27 us
    ppermute x1, starting transfers between devices, padded(): lax.ppermute(lax.slice_in_dim(block, 0, width, axis=dim), axis, backward)  8.23 us
    gather x4, local copies, waits for them, and re-layouts, step(): picked = cand[idx].reshape(sd, slot_width, width, incid)  5.95 us
    all_to_all x1, starting transfers between devices, summed_on_arrival(): lax.all_to_all(blocks, axis, split_axis=0, concat_axis=0, tiled=True)  4.99 us
  transfers between devices with their start and end apart: 4, of which 2 were waited for; matrix products, arithmetic and copies ran while one was open for 30% of the time, Pallas kernels for 0%

commit v1 on v0

v1 whole, which is shorter than its diff:
```python
import jax
import jax.numpy as jnp
from jax import lax
from jax.experimental import pallas as pl
from jax.experimental.pallas import tpu as pltpu
from jax.sharding import PartitionSpec as P

F32 = jnp.float32
BF16 = jnp.bfloat16
NBG = 2
LANES = 128
HALF = 64


def dot(a, b, ca=1, cb=0):
    return lax.dot_general(a, b, (((ca,), (cb,)), ((), ())), preferred_element_type=F32)


def params():
    return pltpu.CompilerParams(vmem_limit_bytes=48 * 1024 * 1024)


def to_planes(rows, planes, base):
    sd, width = rows.shape
    for t in range(width // LANES):
        planes[pl.ds(base * HALF + t, sd, stride=HALF), :] = rows[:, t * LANES:(t + 1) * LANES].astype(F32)


def pack_kernel(x, boxes, out):
    ngrp = out.shape[0]
    feat = x.shape[1] // ngrp
    tag = boxes[...]
    for g in range(ngrp):
        out[g, :, :feat] = x[:, g * feat:(g + 1) * feat]
        out[g, :, feat:] = tag


def pack(coeffs, boxes, ngrp):
    sd, width = coeffs.shape
    tag = jnp.broadcast_to(boxes.astype(BF16)[:, None], (sd, LANES))
    return pl.pallas_call(
        pack_kernel,
        out_shape=jax.ShapeDtypeStruct((ngrp, sd, width // ngrp + LANES), BF16),
        compiler_params=params(),
        name="pack",
    )(coeffs, tag)


def sums_kernel(got, out, onehot, *, nbc):
    n, sd, wide = got.shape
    feat = wide - LANES
    flat = got[...].reshape(n * sd, wide)
    box = flat[:, feat:feat + nbc].astype(F32)
    ids = lax.broadcasted_iota(jnp.int32, (n * sd, nbc), 1).astype(F32)
    hot = (box == ids).astype(F32).astype(BF16)
    onehot[...] = hot
    sums = dot(hot, flat[:, :feat], 0, 0).astype(BF16)
    for c in range(out.shape[0]):
        out[c] = sums


def box_sums(got, nbc, ncell):
    n, sd, wide = got.shape
    import functools
    return pl.pallas_call(
        functools.partial(sums_kernel, nbc=nbc),
        out_shape=(
            jax.ShapeDtypeStruct((ncell, nbc, wide - LANES), BF16),
            jax.ShapeDtypeStruct((n * sd, nbc), BF16),
        ),
        compiler_params=params(),
        name="box_sums",
    )(got)


def rows_kernel(column, onehot, coupling, out):
    out[...] = dot(onehot[...], coupling[...]).astype(BF16)


def sphere_rows(column, onehot, coupling):
    n, nbc = onehot.shape
    nbox = coupling.shape[1]
    return pl.pallas_call(
        rows_kernel,
        out_shape=jax.ShapeDtypeStruct((n, nbox), BF16),
        grid_spec=pltpu.PrefetchScalarGridSpec(
            num_scalar_prefetch=1,
            grid=(1,),
            in_specs=[
                pl.BlockSpec((n, nbc), lambda i, c: (0, 0)),
                pl.BlockSpec((nbc, nbox), lambda i, c: (c[0], 0)),
            ],
            out_specs=pl.BlockSpec((n, nbox), lambda i, c: (0, 0)),
        ),
        compiler_params=params(),
        name="sphere_rows",
    )(column, onehot, coupling)


def couple_kernel(rows, sums, out):
    nbox = rows.shape[1]
    feat = sums.shape[2]
    n, sd = out.shape[0], out.shape[1]
    out[...] = dot(rows[...], sums[...].reshape(nbox, feat)).astype(BF16).reshape(n, sd, feat)


def couple(rows, sums, n, sd):
    return pl.pallas_call(
        couple_kernel,
        out_shape=jax.ShapeDtypeStruct((n, sd, sums.shape[2]), BF16),
        compiler_params=params(),
        name="couple",
    )(rows, sums)


def swap_halves(a):
    return pltpu.roll(a, HALF, 1)


def near_kernel(nbr, low, own, high, scale, rot, perm, out, planes, cand, turn, diag, total):
    slots, sd, _ = scale.shape
    width = rot.shape[1]
    tiles = low.shape[1] // LANES
    lane = lax.broadcasted_iota(jnp.int32, (HALF, LANES), 1) < HALF
    turn[...] = jnp.zeros_like(turn)
    diag[...] = jnp.zeros_like(diag)
    for k in range(slots):
        turn[k * LANES:k * LANES + width, :] = dot(rot[k], perm[...]).astype(BF16)
    planes[...] = jnp.zeros_like(planes)
    for c, part in enumerate((low, own, high)):
        to_planes(part, planes, 0)
        for s in range(0, sd, 2):
            both = planes[s * HALF:(s + 2) * HALF, :].T
            top, bottom = both[:HALF], both[HALF:]
            cand[c * sd + s] = jnp.where(lane, top, swap_halves(bottom)).astype(BF16)
            cand[c * sd + s + 1] = jnp.where(lane, swap_halves(top), bottom).astype(BF16)
    total[...] = jnp.zeros_like(total)
    group = 4

    def step(q, carry):
        k = 2 * q
        r = pl.multiple_of(q * 2 * LANES, 2 * LANES)
        diag[:LANES, :LANES] = turn[pl.ds(r, LANES), :]
        diag[LANES:, LANES:] = turn[pl.ds(r + LANES, LANES), :]
        fact0 = scale[k]
        fact1 = scale[k + 1]
        back = turn[pl.ds(r, 2 * LANES), :]
        fwd = diag[...]
        for g in range(sd // group):
            picked = []
            for s in range(g * group, (g + 1) * group):
                a = cand[nbr[s, k]]
                b = cand[nbr[s, k + 1]]
                picked.append(jnp.concatenate([a, b], axis=1))
            turned = dot(jnp.concatenate(picked, axis=0), fwd, 1, 1)
            scaled = []
            for n, s in enumerate(range(g * group, (g + 1) * group)):
                f = jnp.concatenate([fact0[s:s + 1], fact1[s:s + 1]], axis=1)
                scaled.append((turned[n * HALF:(n + 1) * HALF] * f).astype(BF16))
            rows = pl.ds(g * group * HALF, group * HALF)
            total[rows, :] += dot(jnp.concatenate(scaled, axis=0), back)
        return carry

    lax.fori_loop(0, slots // 2, step, 0)
    for s in range(0, sd, 2):
        a = total[s * HALF:(s + 1) * HALF, :]
        b = total[(s + 1) * HALF:(s + 2) * HALF, :]
        top = jnp.where(lane, a, swap_halves(b))
        bottom = jnp.where(lane, swap_halves(a), b)
        out[s * HALF:(s + 2) * HALF, :] = jnp.concatenate([top, bottom], axis=0).T


def near_field(nbr, low, own, high, scale, rot, perm):
    slots, sd, _ = scale.shape
    vmem = pl.BlockSpec(memory_space=pltpu.VMEM)
    return pl.pallas_call(
        near_kernel,
        out_shape=jax.ShapeDtypeStruct((sd * HALF, LANES), F32),
        in_specs=[pl.BlockSpec(memory_space=pltpu.SMEM)] + [vmem] * 6,
        out_specs=vmem,
        scratch_shapes=[
            pltpu.VMEM((sd * HALF, LANES), F32),
            pltpu.VMEM((3 * sd, HALF, LANES), BF16),
            pltpu.VMEM((slots * LANES, LANES), BF16),
            pltpu.VMEM((2 * LANES, 2 * LANES), BF16),
            pltpu.VMEM((sd * HALF, LANES), F32),
        ],
        compiler_params=params(),
        name="near",
    )(nbr, low, own, high, scale, rot, perm)


def tail_kernel(got, near, x, tmat_re, tmat_im, maps, out, planes):
    ngrp, sd, feat = got.shape
    per = feat // LANES
    lane = lax.broadcasted_iota(jnp.int32, (HALF, LANES), 1) < HALF
    half = tmat_re.shape[1]
    planes[...] = jnp.zeros_like(planes)
    for g in range(ngrp):
        part = got[g]
        for q in range(per):
            t = g * per + q
            planes[pl.ds(t, sd, stride=HALF), :] = part[:, q * LANES:(q + 1) * LANES].astype(F32)
    hi = maps[:LANES]
    lo = maps[LANES:]
    for s in range(sd):
        loc = planes[s * HALF:(s + 1) * HALF, :]
        both = jnp.concatenate([loc, swap_halves(loc)], axis=0).astype(BF16)
        prod = dot(hi, both) + dot(lo, both)
        field = near[s * HALF:(s + 1) * HALF, :] + jnp.where(lane, prod[:HALF], prod[HALF:])
        ur, ui = field[:half], field[half:2 * half]
        tr, ti = tmat_re[s], tmat_im[s]
        planes[s * HALF:s * HALF + half, :] = tr * ur - ti * ui
        planes[s * HALF + half:s * HALF + 2 * half, :] = tr * ui + ti * ur
    for t in range(2 * half):
        cols = slice(t * LANES, (t + 1) * LANES)
        out[:, cols] = (x[:, cols].astype(F32) - planes[pl.ds(t, sd, stride=HALF), :]).astype(BF16)


def tail(got, near, coeffs, tmat_re, tmat_im, maps):
    sd = coeffs.shape[0]
    return pl.pallas_call(
        tail_kernel,
        out_shape=jax.ShapeDtypeStruct(coeffs.shape, BF16),
        scratch_shapes=[pltpu.VMEM((sd * HALF, LANES), F32)],
        compiler_params=params(),
        name="tail",
    )(got, near, coeffs, tmat_re, tmat_im, maps)


def plane_maps(out_map, in_map):
    both = jnp.dot(in_map.astype(F32), out_map.astype(F32), precision=lax.Precision.HIGHEST)
    n = both.shape[0] // 2
    m = both.reshape(n, 2, n, 2)
    pad = ((0, HALF - n), (0, HALF - n))
    ee, eo, oe, oo = (jnp.pad(m[:, i, :, j], pad) for i in (0, 1) for j in (0, 1))
    top = jnp.concatenate([ee, eo], axis=1)
    bottom = jnp.concatenate([oo, oe], axis=1)
    full = jnp.concatenate([top, bottom], axis=0)
    hi = lax.reduce_precision(full, 8, 7)
    return jnp.concatenate([hi, full - hi], axis=0).astype(BF16)


def shards(coeffs, neighbours, counts, boxes, axial, rotations, out_map, coupling, in_map, tmat):
    sd, total = coeffs.shape
    width = rotations.shape[1]
    slots = neighbours.shape[1]
    ngrp = lax.axis_size("grp")
    ncell = lax.axis_size("cells")
    nbc = NBG * ngrp
    forward = [(i, i + 1) for i in range(ncell - 1)]
    backward = [(b, a) for a, b in forward]
    low = lax.ppermute(coeffs, "cells", forward)
    high = lax.ppermute(coeffs, "cells", backward)

    sent = pack(coeffs, boxes, ngrp)
    got = lax.all_to_all(sent, "grp", 0, 0, tiled=True)
    sums, onehot = box_sums(got, nbc, ncell)
    every = lax.all_to_all(sums, "cells", 0, 0, tiled=True)
    column = lax.axis_index("cells").astype(jnp.int32)[None]
    rows = sphere_rows(column, onehot, coupling)

    live = lax.broadcasted_iota(jnp.int32, (sd, slots), 1) < counts[:, None]
    scale = jnp.where(live[:, :, None], axial.astype(F32), 0.0).transpose(1, 0, 2)
    scale = jnp.pad(scale, ((0, 0), (0, 0), (0, LANES - width)))
    spot = jnp.arange(width, dtype=jnp.int32)
    spot = (spot % 2) * HALF + spot // 2
    perm = (spot[:, None] == jnp.arange(LANES, dtype=jnp.int32)[None, :]).astype(BF16)
    near = near_field(neighbours, low, coeffs, high, scale, rotations, perm)

    local = couple(rows, every, ngrp, sd)
    mine = lax.all_to_all(local, "grp", 0, 0, tiled=True)
    spread = jnp.repeat(tmat.reshape(sd, width // 2, 2), HALF, axis=2)
    quarter = width // 4
    return tail(mine, near, coeffs, spread[:, :quarter], spread[:, quarter:], plane_maps(out_map, in_map))


def solution(mesh):
    rows = P(("cells", "grp"), None)
    flat = P(("cells", "grp"))
    in_specs = (rows, rows, flat, flat, P(("cells", "grp"), None, None), P(), P(), P(), P(), rows)
    return jax.shard_map(shards, mesh=mesh, in_specs=in_specs, out_specs=rows, check_vma=False)
```

time: 152 us -> 77.3 us (0.51)
  the two profiles are of different devices: /device:TPU:8 before, /device:TPU:1 now
where the time goes in v1:
time: 77.3 us; the launch traced here: 76.7 us
  starting transfers between devices  32.4 us (42%)
  Pallas kernels  18.2 us (24%)
  waiting for transfers between devices  12.1 us (16%)
  local copies, waits for them, and re-layouts  11.8 us (15%)
  other arithmetic  1 us (1%)
  matrix products  0.87 us (1%)
    pallas_call x1, Pallas kernels, near_field(): pl.pallas_call(near_kernel, out_shape=jax.ShapeDtypeStruct((sd * HALF, LA...  13.8 us
    all_to_all x1, waiting for transfers between devices, shards(): every = lax.all_to_all(sums, 'cells', 0, 0, tiled=True)  11 us
    all_to_all x1, starting transfers between devices, shards(): every = lax.all_to_all(sums, 'cells', 0, 0, tiled=True)  10.4 us
    all_to_all x1, starting transfers between devices, shards(): mine = lax.all_to_all(local, 'grp', 0, 0, tiled=True)  8.3 us
    all_to_all x1, starting transfers between devices, shards(): got = lax.all_to_all(sent, 'grp', 0, 0, tiled=True)  6.62 us
    unnamed x27, local copies, waits for them, and re-layouts  5.89 us
    ppermute x1, starting transfers between devices, shards(): low = lax.ppermute(coeffs, 'cells', forward)  5.85 us
    slice x1, local copies, waits for them, and re-layouts, plane_maps(): m[:, i, :, j]  2.84 us
  transfers between devices with their start and end apart: 5, of which 2 were waited for; matrix products, arithmetic and copies ran while one was open for 16% of the time, Pallas kernels for 22%

profile of v1, /device:TPU:1, one launch (start us, length us, event | category | flops | bytes accessed | tf_op | source)
XLA Modules:
  0.0 76.7 jit_solution(9954111311445644702)
XLA Ops:
  0.0 0.0 copy-start
  0.0 5.8 %collective-permute-start = (bf16[16,6144]{1,0:T(8,128)(2,1)}, bf16[16,6144]{1,0:T(8,128)(2,1)S(1)}, u32[]{:S(2)}, u32[]{:S(2)}) collective-permute-start(bf16[16,6144]{1,0:T(8,128)(2,1)} %x.13), channel_id=1, source_target_pairs={{0,16},{16,32},{32,48},{48,64},{64,80},{80,96},{96,112},{112,128},... | collective-permute-start | bytes 589832 | tf_op jit(solution)/shard_map/ppermute | solution.py:253
  5.9 1.3 %collective-permute-start.1 = (bf16[16,6144]{1,0:T(8,128)(2,1)}, bf16[16,6144]{1,0:T(8,128)(2,1)S(1)}, u32[]{:S(2)}, u32[]{:S(2)}) collective-permute-start(bf16[16,6144]{1,0:T(8,128)(2,1)} %x.13), channel_id=1, source_target_pairs={{16,0},{32,16},{48,32},{64,48},{80,64},{96,80},{112,96},{128,112},... | collective-permute-start | bytes 589832 | tf_op jit(solution)/shard_map/ppermute | solution.py:254
  7.2 0.7 convert_element_type.19
  7.8 0.1 broadcast_in_dim.29.boxes
  7.9 0.9 %copy-done.1 = bf16[16,6144]{1,0:T(8,128)(2,1)S(1)} copy-done((bf16[16,6144]{1,0:T(8,128)(2,1)S(1)}, bf16[16,6144]{1,0:T(8,128)(2,1)}, u32[]{:S(2)}) %copy-start.1) | copy-done | bytes 196632
  8.8 0.7 pack.1
  9.6 6.6 %all-to-all-start = ((bf16[16,16,512]{2,1,0:T(8,128)(2,1)}), bf16[16,16,512]{2,1,0:T(8,128)(2,1)S(1)}, u32[]{:S(2)}, u32[]{:S(2)}) async-start(bf16[16,16,512]{2,1,0:T(8,128)(2,1)} %pack.1), calls=%async_computation | async-start | bytes 524288 | tf_op jit(solution)/shard_map/all_to_all | solution.py:257
  16.2 0.0 copy-done
  16.2 0.9 %fusion.12 = f32[96,96]{1,0:T(8,128)S(1)} fusion(bf16[96,96]{1,0:T(8,128)(2,1)S(1)} %copy-done, bf16[96,96]{1,0:T(8,128)(2,1)} %param.16), kind=kOutput, calls=%fused_computation.28 | convolution fusion | flops 1769472 | bytes 73728 | tf_op jit(solution)/shard_map/dot_general | solution.py:232
  17.1 1.2 %reshape.53 = f32[48,2,48,2]{3,2,1,0:T(8,128)S(1)} reshape(f32[96,96]{1,0:T(8,128)S(1)} %fusion.12) | data formatting | bytes 73728 | tf_op jit(solution)/shard_map/reshape | solution.py:234
  18.3 2.8 %fusion.10 = (f32[48,1,48,1]{3,2,1,0:T(8,128)}, f32[48,1,48,1]{3,2,1,0:T(8,128)}, f32[48,1,48,1]{3,2,1,0:T(8,128)}, f32[48,1,48,1]{3,2,1,0:T(8,128)}) fusion(f32[48,2,48,2]{3,2,1,0:T(8,128)S(1)} %reshape.53), kind=kLoop, calls=%fused_computation.26 | loop fusion | bytes 73728 | tf_op jit(solution)/shard_map/slice | solution.py:236
  21.1 1.8 %copy.19 = f32[48,1,48,1]{2,0,3,1:T(8,128)S(1)} copy(f32[48,1,48,1]{3,2,1,0:T(8,128)} %get-tuple-element.11) | data formatting | bytes 18432
  22.9 0.0 copy-start.6
  22.9 1.8 %copy.20 = f32[48,1,48,1]{2,0,3,1:T(8,128)S(1)} copy(f32[48,1,48,1]{3,2,1,0:T(8,128)} %get-tuple-element.13) | data formatting | bytes 18432
  24.7 0.0 copy-done.7
  24.7 0.0 copy-start.10
  24.7 0.4 copy.21
  25.2 0.0 copy-done.6
  25.2 0.0 copy-start.9
  25.2 0.4 copy.22
  25.6 0.0 copy-done.10
  25.6 1.1 %all-to-all-done.got = bf16[16,16,512]{2,1,0:T(8,128)(2,1)S(1)} async-done(((bf16[16,16,512]{2,1,0:T(8,128)(2,1)}), bf16[16,16,512]{2,1,0:T(8,128)(2,1)S(1)}, u32[]{:S(2)}, u32[]{:S(2)}) %all-to-all-start) | async-done | bytes 262176 | tf_op jit(solution)/shard_map/all_to_all | solution.py:257
  26.8 1.0 %box_sums.1 = (bf16[16,32,384]{2,1,0:T(8,128)(2,1)}, bf16[256,32]{1,0:T(8,128)(2,1)S(1)}) custom-call(bf16[16,16,512]{2,1,0:T(8,128)(2,1)S(1)} %all-to-all-done.got), custom_call_target="tpu_custom_call" | custom-call | tf_op jit(solution)/shard_map/box_sums/pallas_call | solution.py:65
  27.8 10.4 %all-to-all-start.1 = ((bf16[16,32,384]{2,1,0:T(8,128)(2,1)}), bf16[16,32,384]{2,1,0:T(8,128)(2,1)S(1)}, u32[]{:S(2)}, u32[]{:S(2)}) async-start(bf16[16,32,384]{2,1,0:T(8,128)(2,1)} %get-tuple-element.8), calls=%async_computation.1 | async-start | bytes 786432 | tf_op jit(solution)/shard_map/all_to_all | solution.py:259
  38.1 0.1 reduce-precision_convert_fusion
  38.2 0.0 copy-done.9
  38.2 0.1 copy.13
  38.3 0.4 copy.14
  38.7 0.0 copy-start.8
  38.7 1.0 %broadcast_in_dim.32 = f32[16,48,2,64]{3,2,1,0:T(2,128)S(1)} broadcast(f32[16,48,2]{2,1,0:T(8,128)S(1)} %copy.14), dimensions={0,1,2} | broadcast | bytes 399360 | tf_op jit(solution)/shard_map/broadcast_in_dim | solution.py:273
  39.7 0.0 copy-start.4
  39.7 0.4 reshape.52
  40.2 0.0 copy-done.8
  40.2 0.1 select_bitcast_fusion
  40.3 0.4 copy-done.4
  40.7 0.2 sphere_rows.1.rows
  40.9 11.0 %all-to-all-done.1.sums = bf16[16,32,384]{2,1,0:T(8,128)(2,1)S(1)} async-done(((bf16[16,32,384]{2,1,0:T(8,128)(2,1)}), bf16[16,32,384]{2,1,0:T(8,128)(2,1)S(1)}, u32[]{:S(2)}, u32[]{:S(2)}) %all-to-all-start.1) | async-done | bytes 393248 | tf_op jit(solution)/shard_map/all_to_all | solution.py:259
  51.9 1.0 %couple.1 = bf16[16,16,384]{2,1,0:T(8,128)(2,1)} custom-call(bf16[256,512]{1,0:T(8,128)(2,1)S(1)} %sphere_rows.1.rows, bf16[16,32,384]{2,1,0:T(8,128)(2,1)S(1)} %all-to-all-done.1.sums), custom_call_target="tpu_custom_call" | custom-call | tf_op jit(solution)/shard_map/couple/pallas_call | solution.py:108
  52.9 8.3 %all-to-all-start.2 = ((bf16[16,16,384]{2,1,0:T(8,128)(2,1)}), bf16[16,16,384]{2,1,0:T(8,128)(2,1)S(1)}, u32[]{:S(2)}, u32[]{:S(2)}) async-start(bf16[16,16,384]{2,1,0:T(8,128)(2,1)} %couple.1), calls=%async_computation.2 | async-start | bytes 393216 | tf_op jit(solution)/shard_map/all_to_all | solution.py:272
  61.2 0.1 fusion.6.perm
  61.3 0.0 collective-permute-done.low
  61.3 0.0 collective-permute-done.1.high
  61.3 0.0 copy-done.2
  61.4 0.0 copy-done.3
  61.4 13.8 %near.1 = f32[1024,128]{1,0:T(8,128)S(1)} custom-call(s32[16,32]{1,0:T(8,128)S(1)} %copy-done.5, bf16[16,6144]{1,0:T(8,128)(2,1)S(1)} %collective-permute-done.low, bf16[16,6144]{1,0:T(8,128)(2,1)S(1)} %copy-done.2, bf16[16,6144]{1,0:T(8,128)(2,1)S(1)} %collective-permute-done.1.high, f32[32,16,128]{2,1,0:T(8,128)S(1)} %pad.17.scale, ...), custom_call_target="tpu_custom_call" | custom-call | tf_op jit(solution)/shard_map/near/pallas_call | solution.py:176
  75.2 0.0 all-to-all-done.2.got
  75.2 1.5 %tail.1 = bf16[16,6144]{1,0:T(8,128)(2,1)} custom-call(bf16[16,16,384]{2,1,0:T(8,128)(2,1)S(1)} %all-to-all-done.2.got, f32[1024,128]{1,0:T(8,128)S(1)} %near.1, bf16[16,6144]{1,0:T(8,128)(2,1)S(1)} %copy-done.2, f32[16,24,128]{2,1,0:T(8,128)S(1)} %get-tuple-element.16.tmat_re, f32[16,24,128]{2,1,0:T(8,128)S(1)} %get-tuple-element.15.tmat_im, ...), custom_call_target="tpu_custom_call" | custom-call | tf_op jit(solution)/shard_map/tail/pallas_call | solution.py:222
  (12 shorter events, 0.1 us)
Async XLA Ops:
  0.0 16.2 %copy-start = (bf16[96,96]{1,0:T(8,128)(2,1)S(1)}, bf16[96,96]{1,0:T(8,128)(2,1)}, u32[]{:S(2)}) copy-start(bf16[96,96]{1,0:T(8,128)(2,1)} %param.18) | copy-start | bytes 55300
  0.0 61.3 %collective-permute-start = (bf16[16,6144]{1,0:T(8,128)(2,1)}, bf16[16,6144]{1,0:T(8,128)(2,1)S(1)}, u32[]{:S(2)}, u32[]{:S(2)}) collective-permute-start(bf16[16,6144]{1,0:T(8,128)(2,1)} %x.13), channel_id=1, source_target_pairs={{0,16},{16,32},{32,48},{48,64},{64,80},{80,96},{96,112},{112,128},... | collective-permute-start | bytes 589832 | tf_op jit(solution)/shard_map/ppermute | solution.py:253
  5.9 55.5 %collective-permute-start.1 = (bf16[16,6144]{1,0:T(8,128)(2,1)}, bf16[16,6144]{1,0:T(8,128)(2,1)S(1)}, u32[]{:S(2)}, u32[]{:S(2)}) collective-permute-start(bf16[16,6144]{1,0:T(8,128)(2,1)} %x.13), channel_id=1, source_target_pairs={{16,0},{32,16},{48,32},{64,48},{80,64},{96,80},{112,96},{128,112},... | collective-permute-start | bytes 589832 | tf_op jit(solution)/shard_map/ppermute | solution.py:254
  7.9 0.9 %copy-start.1 = (bf16[16,6144]{1,0:T(8,128)(2,1)S(1)}, bf16[16,6144]{1,0:T(8,128)(2,1)}, u32[]{:S(2)}) copy-start(bf16[16,6144]{1,0:T(8,128)(2,1)} %x.13) | copy-start | bytes 589828
  9.6 17.2 %all-to-all-start = ((bf16[16,16,512]{2,1,0:T(8,128)(2,1)}), bf16[16,16,512]{2,1,0:T(8,128)(2,1)S(1)}, u32[]{:S(2)}, u32[]{:S(2)}) async-start(bf16[16,16,512]{2,1,0:T(8,128)(2,1)} %pack.1), calls=%async_computation | async-start | bytes 524288 | tf_op jit(solution)/shard_map/all_to_all | solution.py:257
  21.1 3.6 %copy-start.7 = (f32[48,1,48,1]{3,2,1,0:T(8,128)S(1)}, f32[48,1,48,1]{3,2,1,0:T(8,128)}, u32[]{:S(2)}) copy-start(f32[48,1,48,1]{3,2,1,0:T(8,128)} %get-tuple-element.12) | copy-start | bytes 27652
  22.9 2.3 %copy-start.6 = (f32[48,1,48,1]{3,2,1,0:T(8,128)S(1)}, f32[48,1,48,1]{3,2,1,0:T(8,128)}, u32[]{:S(2)}) copy-start(f32[48,1,48,1]{3,2,1,0:T(8,128)} %get-tuple-element.14) | copy-start | bytes 27652
  24.7 0.9 %copy-start.10 = (s32[16]{0:T(128)S(1)}, s32[16]{0:T(128)}, u32[]{:S(2)}) copy-start(s32[16]{0:T(128)} %param.12) | copy-start | bytes 196
  25.2 13.1 %copy-start.9 = (f32[16,96]{1,0:T(8,128)S(1)}, f32[16,96]{1,0:T(8,128)}, u32[]{:S(2)}) copy-start(f32[16,96]{1,0:T(8,128)} %param.19) | copy-start | bytes 18436
  27.8 24.2 %all-to-all-start.1 = ((bf16[16,32,384]{2,1,0:T(8,128)(2,1)}), bf16[16,32,384]{2,1,0:T(8,128)(2,1)S(1)}, u32[]{:S(2)}, u32[]{:S(2)}) async-start(bf16[16,32,384]{2,1,0:T(8,128)(2,1)} %get-tuple-element.8), calls=%async_computation.1 | async-start | bytes 786432 | tf_op jit(solution)/shard_map/all_to_all | solution.py:259
  38.7 1.5 %copy-start.8 = (bf16[16,32,96]{2,1,0:T(8,128)(2,1)S(1)}, bf16[16,32,96]{2,1,0:T(8,128)(2,1)}, u32[]{:S(2)}) copy-start(bf16[16,32,96]{2,1,0:T(8,128)(2,1)} %param.14) | copy-start | bytes 294916
  39.7 1.0 %copy-start.4 = (bf16[512,512]{1,0:T(8,128)(2,1)S(1)}, bf16[512,512]{1,0:T(8,128)(2,1)}, u32[]{:S(2)}) copy-start(bf16[512,512]{1,0:T(8,128)(2,1)} %coupling.1) | copy-start | bytes 1572868
  40.7 20.6 %copy-start.2 = (bf16[16,6144]{1,0:T(8,128)(2,1)S(1)}, bf16[16,6144]{1,0:T(8,128)(2,1)}, u32[]{:S(2)}) copy-start(bf16[16,6144]{1,0:T(8,128)(2,1)} %x.13) | copy-start | bytes 589828
  40.7 20.6 %copy-start.3 = (bf16[32,96,96]{2,1,0:T(8,128)(2,1)S(1)}, bf16[32,96,96]{2,1,0:T(8,128)(2,1)}, u32[]{:S(2)}) copy-start(bf16[32,96,96]{2,1,0:T(8,128)(2,1)} %rot.1) | copy-start | bytes 1769476
  40.7 20.6 %copy-start.5 = (s32[16,32]{1,0:T(8,128)S(1)}, s32[16,32]{1,0:T(8,128)}, u32[]{:S(2)}) copy-start(s32[16,32]{1,0:T(8,128)} %nbr.1) | copy-start | bytes 6148
  52.9 22.3 %all-to-all-start.2 = ((bf16[16,16,384]{2,1,0:T(8,128)(2,1)}), bf16[16,16,384]{2,1,0:T(8,128)(2,1)S(1)}, u32[]{:S(2)}, u32[]{:S(2)}) async-start(bf16[16,16,384]{2,1,0:T(8,128)(2,1)} %couple.1), calls=%async_computation.2 | async-start | bytes 393216 | tf_op jit(solution)/shard_map/all_to_all | solution.py:272

commit v2 on v1

--- a/solution.py
+++ b/solution.py
@@ -1,3 +1,5 @@
+import functools
+
 import jax
 import jax.numpy as jnp
 from jax import lax
@@ -5,6 +7,7 @@
 from jax.experimental.pallas import tpu as pltpu
 from jax.sharding import PartitionSpec as P
 
+
 F32 = jnp.float32
 BF16 = jnp.bfloat16
 NBG = 2
@@ -17,13 +20,17 @@
 
 
 def params():
-    return pltpu.CompilerParams(vmem_limit_bytes=48 * 1024 * 1024)
+    return pltpu.CompilerParams(vmem_limit_bytes=12 * 1024 * 1024)
 
 
 def to_planes(rows, planes, base):
     sd, width = rows.shape
     for t in range(width // LANES):
         planes[pl.ds(base * HALF + t, sd, stride=HALF), :] = rows[:, t * LANES:(t + 1) * LANES].astype(F32)
+
+
+def swap_halves(a):
+    return pltpu.roll(a, HALF, 1)
 
 
 def pack_kernel(x, boxes, out):
@@ -61,7 +68,6 @@
 
 def box_sums(got, nbc, ncell):
     n, sd, wide = got.shape
-    import functools
     return pl.pallas_call(
         functools.partial(sums_kernel, nbc=nbc),
         out_shape=(
@@ -113,19 +119,58 @@
     )(rows, sums)
 
 
-def swap_halves(a):
-    return pltpu.roll(a, HALF, 1)
-
-
-def near_kernel(nbr, low, own, high, scale, rot, perm, out, planes, cand, turn, diag, total):
-    slots, sd, _ = scale.shape
-    width = rot.shape[1]
-    tiles = low.shape[1] // LANES
-    lane = lax.broadcasted_iota(jnp.int32, (HALF, LANES), 1) < HALF
+def prep_kernel(counts, axial, rot, perm, permt, out_map, in_map, tmat, turn, scale, maps, tre, tim, cols):
+    sd, slots, width = axial.shape
+    n = width // 2
     turn[...] = jnp.zeros_like(turn)
-    diag[...] = jnp.zeros_like(diag)
     for k in range(slots):
         turn[k * LANES:k * LANES + width, :] = dot(rot[k], perm[...]).astype(BF16)
+    slot = lax.broadcasted_iota(jnp.int32, (slots, LANES), 0)
+    pad = jnp.zeros((slots, LANES - width), F32)
+    for i in range(sd):
+        factor = jnp.concatenate([axial[i].astype(F32), pad], axis=1)
+        scale[pl.ds(i, slots, stride=sd), :] = jnp.where(slot < counts[i], factor, 0.0)
+    both = dot(in_map[...], out_map[...])
+    hi = both.astype(BF16)
+    lo = (both - hi.astype(F32)).astype(BF16)
+    for r, part in enumerate((hi, lo)):
+        moved = dot(dot(permt[...], part).astype(BF16), perm[...])
+        maps[r * LANES:r * LANES + HALF, :] = moved[:HALF].astype(BF16)
+        maps[r * LANES + HALF:(r + 1) * LANES, :] = swap_halves(moved[HALF:]).astype(BF16)
+    cols[...] = tmat[...].T
+    lane = lax.broadcasted_iota(jnp.int32, (n, LANES), 1) < HALF
+    even = cols[pl.ds(0, n, stride=2), :]
+    odd = cols[pl.ds(1, n, stride=2), :]
+    for i in range(sd):
+        row = jnp.where(lane, even[:, i:i + 1], odd[:, i:i + 1])
+        tre[i] = row[:n // 2]
+        tim[i] = row[n // 2:]
+
+
+def prepare(counts, axial, rot, perm, permt, out_map, in_map, tmat):
+    sd, slots, width = axial.shape
+    vmem = pl.BlockSpec(memory_space=pltpu.VMEM)
+    spread = jax.ShapeDtypeStruct((sd, width // 4, LANES), F32)
+    return pl.pallas_call(
+        prep_kernel,
+        out_shape=(
+            jax.ShapeDtypeStruct((slots * LANES, LANES), BF16),
+            jax.ShapeDtypeStruct((slots * sd, LANES), F32),
+            jax.ShapeDtypeStruct((2 * LANES, LANES), BF16),
+            spread,
+            spread,
+        ),
+        in_specs=[pl.BlockSpec(memory_space=pltpu.SMEM)] + [vmem] * 7,
+        scratch_shapes=[pltpu.VMEM((width, sd), F32)],
+        compiler_params=params(),
+        name="prepare",
+    )(counts, axial, rot, perm, permt, out_map, in_map, tmat)
+
+
+def near_kernel(nbr, low, own, high, scale, turn, out, planes, cand, diag, total):
+    sd, slots = nbr.shape
+    lane = lax.broadcasted_iota(jnp.int32, (HALF, LANES), 1) < HALF
+    diag[...] = jnp.zeros_like(diag)
     planes[...] = jnp.zeros_like(planes)
     for c, part in enumerate((low, own, high)):
         to_planes(part, planes, 0)
@@ -142,8 +187,8 @@
         r = pl.multiple_of(q * 2 * LANES, 2 * LANES)
         diag[:LANES, :LANES] = turn[pl.ds(r, LANES), :]
         diag[LANES:, LANES:] = turn[pl.ds(r + LANES, LANES), :]
-        fact0 = scale[k]
-        fact1 = scale[k + 1]
+        fact0 = scale[pl.ds(pl.multiple_of(k * sd, sd), sd), :]
+        fact1 = scale[pl.ds(pl.multiple_of(k * sd + sd, sd), sd), :]
         back = turn[pl.ds(r, 2 * LANES), :]
         fwd = diag[...]
         for g in range(sd // group):
@@ -170,24 +215,23 @@
         out[s * HALF:(s + 2) * HALF, :] = jnp.concatenate([top, bottom], axis=0).T
 
 
-def near_field(nbr, low, own, high, scale, rot, perm):
-    slots, sd, _ = scale.shape
+def near_field(nbr, low, own, high, scale, turn):
+    sd, _ = nbr.shape
     vmem = pl.BlockSpec(memory_space=pltpu.VMEM)
     return pl.pallas_call(
         near_kernel,
         out_shape=jax.ShapeDtypeStruct((sd * HALF, LANES), F32),
-        in_specs=[pl.BlockSpec(memory_space=pltpu.SMEM)] + [vmem] * 6,
+        in_specs=[pl.BlockSpec(memory_space=pltpu.SMEM)] + [vmem] * 5,
         out_specs=vmem,
         scratch_shapes=[
             pltpu.VMEM((sd * HALF, LANES), F32),
             pltpu.VMEM((3 * sd, HALF, LANES), BF16),
-            pltpu.VMEM((slots * LANES, LANES), BF16),
             pltpu.VMEM((2 * LANES, 2 * LANES), BF16),
             pltpu.VMEM((sd * HALF, LANES), F32),
         ],
         compiler_params=params(),
         name="near",
-    )(nbr, low, own, high, scale, rot, perm)
+    )(nbr, low, own, high, scale, turn)
 
 
 def tail_kernel(got, near, x, tmat_re, tmat_im, maps, out, planes):
@@ -228,23 +272,9 @@
     )(got, near, coeffs, tmat_re, tmat_im, maps)
 
 
-def plane_maps(out_map, in_map):
-    both = jnp.dot(in_map.astype(F32), out_map.astype(F32), precision=lax.Precision.HIGHEST)
-    n = both.shape[0] // 2
-    m = both.reshape(n, 2, n, 2)
-    pad = ((0, HALF - n), (0, HALF - n))
-    ee, eo, oe, oo = (jnp.pad(m[:, i, :, j], pad) for i in (0, 1) for j in (0, 1))
-    top = jnp.concatenate([ee, eo], axis=1)
-    bottom = jnp.concatenate([oo, oe], axis=1)
-    full = jnp.concatenate([top, bottom], axis=0)
-    hi = lax.reduce_precision(full, 8, 7)
-    return jnp.concatenate([hi, full - hi], axis=0).astype(BF16)
-
-
 def shards(coeffs, neighbours, counts, boxes, axial, rotations, out_map, coupling, in_map, tmat):
-    sd, total = coeffs.shape
+    sd, _ = coeffs.shape
     width = rotations.shape[1]
-    slots = neighbours.shape[1]
     ngrp = lax.axis_size("grp")
     ncell = lax.axis_size("cells")
     nbc = NBG * ngrp
@@ -252,27 +282,24 @@
     backward = [(b, a) for a, b in forward]
     low = lax.ppermute(coeffs, "cells", forward)
     high = lax.ppermute(coeffs, "cells", backward)
-
     sent = pack(coeffs, boxes, ngrp)
     got = lax.all_to_all(sent, "grp", 0, 0, tiled=True)
+    spot = jnp.arange(width, dtype=jnp.int32)
+    spot = (spot % 2) * HALF + spot // 2
+    lanes = jnp.arange(LANES, dtype=jnp.int32)
+    perm = (spot[:, None] == lanes[None, :]).astype(BF16)
+    permt = (lanes[:, None] == spot[None, :]).astype(BF16)
+    turn, scale, maps, tre, tim = prepare(
+        counts, axial, rotations, perm, permt, out_map, in_map, tmat
+    )
     sums, onehot = box_sums(got, nbc, ncell)
     every = lax.all_to_all(sums, "cells", 0, 0, tiled=True)
     column = lax.axis_index("cells").astype(jnp.int32)[None]
     rows = sphere_rows(column, onehot, coupling)
-
-    live = lax.broadcasted_iota(jnp.int32, (sd, slots), 1) < counts[:, None]
-    scale = jnp.where(live[:, :, None], axial.astype(F32), 0.0).transpose(1, 0, 2)
-    scale = jnp.pad(scale, ((0, 0), (0, 0), (0, LANES - width)))
-    spot = jnp.arange(width, dtype=jnp.int32)
-    spot = (spot % 2) * HALF + spot // 2
-    perm = (spot[:, None] == jnp.arange(LANES, dtype=jnp.int32)[None, :]).astype(BF16)
-    near = near_field(neighbours, low, coeffs, high, scale, rotations, perm)
-
+    near = near_field(neighbours, low, coeffs, high, scale, turn)
     local = couple(rows, every, ngrp, sd)
     mine = lax.all_to_all(local, "grp", 0, 0, tiled=True)
-    spread = jnp.repeat(tmat.reshape(sd, width // 2, 2), HALF, axis=2)
-    quarter = width // 4
-    return tail(mine, near, coeffs, spread[:, :quarter], spread[:, quarter:], plane_maps(out_map, in_map))
+    return tail(mine, near, coeffs, tre, tim, maps)
 
 
 def solution(mesh):

time: 77.3 us -> 66.9 us (0.87)
  blocking collectives: 0 us -> 14.1 us
  local copies, waits for them, and re-layouts: 11.8 us -> 1.63 us
  starting transfers between devices: 32.4 us -> 22.4 us
  waiting for transfers between devices: 12.1 us -> 8.82 us
  matrix products: 0.87 us -> 0 us
    all_to_all x0 -> x1, blocking collectives: none -> 14.1 us  [shards(): got = lax.all_to_all(sent, 'grp', 0, 0, tiled=True)]
    all_to_all x1 -> x0, starting transfers between devices: 6.62 us -> none  [shards(): got = lax.all_to_all(sent, 'grp', 0, 0, tiled=True)]
    unnamed x27 -> x20, local copies, waits for them, and re-layouts: 5.89 us -> 1.55 us
    slice x2 -> x0, local copies, waits for them, and re-layouts: 2.86 us -> none  [the longest x1 2.84 us: plane_maps(): m[:, i, :, j]]
    all_to_all x1, waiting for transfers between devices: 11 us -> 8.81 us  [shards(): every = lax.all_to_all(sums, 'cells', 0, 0, tiled=True)]
    reshape x3 -> x0, local copies, waits for them, and re-layouts: 1.99 us -> none  [the longest x1 1.19 us: plane_maps(): m = both.reshape(n, 2, n, 2)]
    ppermute x1, starting transfers between devices: 5.85 us -> 4.18 us  [shards(): low = lax.ppermute(coeffs, 'cells', forward)]
    all_to_all x1, starting transfers between devices: 8.3 us -> 6.76 us  [shards(): mine = lax.all_to_all(local, 'grp', 0, 0, tiled=True)]
  transfers between devices with their start and end apart: 5 -> 4, of which waited for: 2 -> 1; matrix products, arithmetic and copies ran while one was open for 16% -> 0% of each run, Pallas kernels for 22% -> 24%
where the time goes in v2:
time: 66.9 us; the launch traced here: 66.5 us
  starting transfers between devices  22.4 us (33%)
  Pallas kernels  18.6 us (28%)
  blocking collectives  14.1 us (21%)
  waiting for transfers between devices  8.82 us (13%)
  local copies, waits for them, and re-layouts  1.63 us (2%)
  other arithmetic  0.76 us (1%)
    all_to_all x1, blocking collectives, shards(): got = lax.all_to_all(sent, 'grp', 0, 0, tiled=True)  14.1 us
    pallas_call x1, Pallas kernels, near_field(): pl.pallas_call(near_kernel, out_shape=jax.ShapeDtypeStruct((sd * HALF, LA...  13.5 us
    all_to_all x1, starting transfers between devices, shards(): every = lax.all_to_all(sums, 'cells', 0, 0, tiled=True)  10.2 us
    all_to_all x1, waiting for transfers between devices, shards(): every = lax.all_to_all(sums, 'cells', 0, 0, tiled=True)  8.81 us
    all_to_all x1, starting transfers between devices, shards(): mine = lax.all_to_all(local, 'grp', 0, 0, tiled=True)  6.76 us
    ppermute x1, starting transfers between devices, shards(): low = lax.ppermute(coeffs, 'cells', forward)  4.18 us
    unnamed x20, local copies, waits for them, and re-layouts  1.55 us
    pallas_call x1, Pallas kernels, tail(): pl.pallas_call(tail_kernel, out_shape=jax.ShapeDtypeStruct(coeffs.shape,...  1.49 us
  transfers between devices with their start and end apart: 4, of which 1 were waited for; matrix products, arithmetic and copies ran while one was open for 0% of the time, Pallas kernels for 24%

profile of v2, /device:TPU:1, one launch (start us, length us, event | category | flops | bytes accessed | tf_op | source)
XLA Modules:
  0.0 66.5 jit_solution(13101065531897993963)
XLA Ops:
  0.0 0.7 convert_element_type.9
  0.7 0.1 broadcast_in_dim.5.boxes
  0.7 0.0 copy-start
  0.7 0.9 %copy-done = bf16[16,6144]{1,0:T(8,128)(2,1)S(1)} copy-done((bf16[16,6144]{1,0:T(8,128)(2,1)S(1)}, bf16[16,6144]{1,0:T(8,128)(2,1)}, u32[]{:S(2)}) %copy-start) | copy-done | bytes 196632
  1.7 14.1 %all_to_all.15.got = bf16[16,16,512]{2,1,0:T(8,128)(2,1)S(1)} all-to-all(bf16[16,16,512]{2,1,0:T(8,128)(2,1)S(1)} %pack.1), channel_id=1, replica_groups=mesh['cells'=16,'grp'=16] {'grp'}, dimensions={0} | all-to-all | bytes 524288 | tf_op jit(solution)/shard_map/all_to_all | solution.py:286
  15.8 0.0 copy-start.3
  15.8 1.0 %box_sums.1 = (bf16[16,32,384]{2,1,0:T(8,128)(2,1)}, bf16[256,32]{1,0:T(8,128)(2,1)S(1)}) custom-call(bf16[16,16,512]{2,1,0:T(8,128)(2,1)S(1)} %all_to_all.15.got), custom_call_target="tpu_custom_call" | custom-call | tf_op jit(solution)/shard_map/box_sums/pallas_call | solution.py:71
  16.8 0.0 copy-start.1
  16.8 10.2 %all-to-all-start.1 = ((bf16[16,32,384]{2,1,0:T(8,128)(2,1)}), bf16[16,32,384]{2,1,0:T(8,128)(2,1)S(1)}, u32[]{:S(2)}, u32[]{:S(2)}) async-start(bf16[16,32,384]{2,1,0:T(8,128)(2,1)} %get-tuple-element.13), calls=%async_computation.1 | async-start | bytes 786432 | tf_op jit(solution)/shard_map/all_to_all | solution.py:296
  27.0 0.0 copy-done.1
  27.0 4.2 %collective-permute-start = (bf16[16,6144]{1,0:T(8,128)(2,1)S(1)}, bf16[16,6144]{1,0:T(8,128)(2,1)S(1)}, u32[]{:S(2)}, u32[]{:S(2)}) collective-permute-start(bf16[16,6144]{1,0:T(8,128)(2,1)S(1)} %copy-done.1), channel_id=1, source_target_pairs={{0,16},{16,32},{32,48},{48,64},{64,80},{80,96},{96,112},{112,128},... | collective-permute-start | bytes 589832 | tf_op jit(solution)/shard_map/ppermute | solution.py:283
  31.2 1.3 %collective-permute-start.1 = (bf16[16,6144]{1,0:T(8,128)(2,1)S(1)}, bf16[16,6144]{1,0:T(8,128)(2,1)S(1)}, u32[]{:S(2)}, u32[]{:S(2)}) collective-permute-start(bf16[16,6144]{1,0:T(8,128)(2,1)S(1)} %copy-done.1), channel_id=1, source_target_pairs={{16,0},{32,16},{48,32},{64,48},{80,64},{96,80},{112,96},{128,112},... | collective-permute-start | bytes 589832 | tf_op jit(solution)/shard_map/ppermute | solution.py:284
  32.5 0.0 copy-done.3
  32.5 0.2 sphere_rows.1.rows
  32.7 0.0 copy-start.2
  32.7 8.8 %all-to-all-done.1.sums = bf16[16,32,384]{2,1,0:T(8,128)(2,1)S(1)} async-done(((bf16[16,32,384]{2,1,0:T(8,128)(2,1)}), bf16[16,32,384]{2,1,0:T(8,128)(2,1)S(1)}, u32[]{:S(2)}, u32[]{:S(2)}) %all-to-all-start.1) | async-done | bytes 393248 | tf_op jit(solution)/shard_map/all_to_all | solution.py:296
  41.5 1.0 %couple.1 = bf16[16,16,384]{2,1,0:T(8,128)(2,1)} custom-call(bf16[256,512]{1,0:T(8,128)(2,1)S(1)} %sphere_rows.1.rows, bf16[16,32,384]{2,1,0:T(8,128)(2,1)S(1)} %all-to-all-done.1.sums), custom_call_target="tpu_custom_call" | custom-call | tf_op jit(solution)/shard_map/couple/pallas_call | solution.py:114
  42.5 0.0 copy-start.4
  42.5 6.8 %all-to-all-start.2 = ((bf16[16,16,384]{2,1,0:T(8,128)(2,1)}), bf16[16,16,384]{2,1,0:T(8,128)(2,1)S(1)}, u32[]{:S(2)}, u32[]{:S(2)}) async-start(bf16[16,16,384]{2,1,0:T(8,128)(2,1)} %couple.1), calls=%async_computation.2 | async-start | bytes 393216 | tf_op jit(solution)/shard_map/all_to_all | solution.py:301
  49.3 0.0 copy-start.5
  49.3 0.0 copy-start.6
  49.3 0.0 copy-start.7
  49.3 0.0 copy-start.9
  49.3 0.1 fusion.1.perm
  49.4 0.0 copy-done.2
  49.4 0.0 copy-done.4
  49.4 0.6 copy-done.5
  50.0 0.0 copy-done.6
  50.0 0.0 copy-done.7
  50.0 0.0 copy-done.9
  50.0 0.0 copy-start.8
  50.0 1.4 %prepare.1 = (bf16[4096,128]{1,0:T(8,128)(2,1)S(1)}, f32[512,128]{1,0:T(8,128)S(1)}, bf16[256,128]{1,0:T(8,128)(2,1)S(1)}, f32[16,24,128]{2,1,0:T(8,128)S(1)}, f32[16,24,128]{2,1,0:T(8,128)S(1)}) custom-call(s32[16]{0:T(128)S(1)} %copy-done.9, bf16[16,32,96]{2,1,0:T(8,128)(2,1)S(1)} %copy-done.4, bf16[32,96,96]{2,1,0:T(8,128)(2,1)S(1)} %copy-done.2, ...), custom_call_target="tpu_custom_call" | custom-call | tf_op jit(solution)/shard_map/prepare/pallas_call | solution.py:154
  51.5 0.0 collective-permute-done.low
  51.5 0.0 collective-permute-done.1.high
  51.5 0.0 copy-done.8
  51.5 13.5 %near.1 = f32[1024,128]{1,0:T(8,128)S(1)} custom-call(s32[16,32]{1,0:T(8,128)S(1)} %copy-done.8, bf16[16,6144]{1,0:T(8,128)(2,1)S(1)} %collective-permute-done.low, bf16[16,6144]{1,0:T(8,128)(2,1)S(1)} %copy-done.1, bf16[16,6144]{1,0:T(8,128)(2,1)S(1)} %collective-permute-done.1.high, f32[512,128]{1,0:T(8,128)S(1)} %get-tuple-element.14.scale, ...), custom_call_target="tpu_custom_call" | custom-call | tf_op jit(solution)/shard_map/near/pallas_call | solution.py:221
  65.0 0.0 all-to-all-done.2.got
  65.0 1.5 %tail.1 = bf16[16,6144]{1,0:T(8,128)(2,1)} custom-call(bf16[16,16,384]{2,1,0:T(8,128)(2,1)S(1)} %all-to-all-done.2.got, f32[1024,128]{1,0:T(8,128)S(1)} %near.1, bf16[16,6144]{1,0:T(8,128)(2,1)S(1)} %copy-done.1, f32[16,24,128]{2,1,0:T(8,128)S(1)} %get-tuple-element.16.tmat_re, f32[16,24,128]{2,1,0:T(8,128)S(1)} %get-tuple-element.17.tmat_im, ...), custom_call_target="tpu_custom_call" | custom-call | tf_op jit(solution)/shard_map/tail/pallas_call | solution.py:266
  (3 shorter events, 0.0 us)
Async XLA Ops:
  0.7 0.9 %copy-start = (bf16[16,6144]{1,0:T(8,128)(2,1)S(1)}, bf16[16,6144]{1,0:T(8,128)(2,1)}, u32[]{:S(2)}) copy-start(bf16[16,6144]{1,0:T(8,128)(2,1)} %x.3) | copy-start | bytes 589828
  15.8 16.6 %copy-start.3 = (bf16[512,512]{1,0:T(8,128)(2,1)S(1)}, bf16[512,512]{1,0:T(8,128)(2,1)}, u32[]{:S(2)}) copy-start(bf16[512,512]{1,0:T(8,128)(2,1)} %coupling.1) | copy-start | bytes 1572868
  16.8 10.2 %copy-start.1 = (bf16[16,6144]{1,0:T(8,128)(2,1)S(1)}, bf16[16,6144]{1,0:T(8,128)(2,1)}, u32[]{:S(2)}) copy-start(bf16[16,6144]{1,0:T(8,128)(2,1)} %x.3) | copy-start | bytes 589828
  16.8 24.7 %all-to-all-start.1 = ((bf16[16,32,384]{2,1,0:T(8,128)(2,1)}), bf16[16,32,384]{2,1,0:T(8,128)(2,1)S(1)}, u32[]{:S(2)}, u32[]{:S(2)}) async-start(bf16[16,32,384]{2,1,0:T(8,128)(2,1)} %get-tuple-element.13), calls=%async_computation.1 | async-start | bytes 786432 | tf_op jit(solution)/shard_map/all_to_all | solution.py:296
  27.0 24.5 %collective-permute-start = (bf16[16,6144]{1,0:T(8,128)(2,1)S(1)}, bf16[16,6144]{1,0:T(8,128)(2,1)S(1)}, u32[]{:S(2)}, u32[]{:S(2)}) collective-permute-start(bf16[16,6144]{1,0:T(8,128)(2,1)S(1)} %copy-done.1), channel_id=1, source_target_pairs={{0,16},{16,32},{32,48},{48,64},{64,80},{80,96},{96,112},{112,128},... | collective-permute-start | bytes 589832 | tf_op jit(solution)/shard_map/ppermute | solution.py:283
  31.2 20.3 %collective-permute-start.1 = (bf16[16,6144]{1,0:T(8,128)(2,1)S(1)}, bf16[16,6144]{1,0:T(8,128)(2,1)S(1)}, u32[]{:S(2)}, u32[]{:S(2)}) collective-permute-start(bf16[16,6144]{1,0:T(8,128)(2,1)S(1)} %copy-done.1), channel_id=1, source_target_pairs={{16,0},{32,16},{48,32},{64,48},{80,64},{96,80},{112,96},{128,112},... | collective-permute-start | bytes 589832 | tf_op jit(solution)/shard_map/ppermute | solution.py:284
  32.7 16.7 %copy-start.2 = (bf16[32,96,96]{2,1,0:T(8,128)(2,1)S(1)}, bf16[32,96,96]{2,1,0:T(8,128)(2,1)}, u32[]{:S(2)}) copy-start(bf16[32,96,96]{2,1,0:T(8,128)(2,1)} %rot.1) | copy-start | bytes 1769476
  42.5 6.9 %copy-start.4 = (bf16[16,32,96]{2,1,0:T(8,128)(2,1)S(1)}, bf16[16,32,96]{2,1,0:T(8,128)(2,1)}, u32[]{:S(2)}) copy-start(bf16[16,32,96]{2,1,0:T(8,128)(2,1)} %axial.1) | copy-start | bytes 294916
  42.5 22.5 %all-to-all-start.2 = ((bf16[16,16,384]{2,1,0:T(8,128)(2,1)}), bf16[16,16,384]{2,1,0:T(8,128)(2,1)S(1)}, u32[]{:S(2)}, u32[]{:S(2)}) async-start(bf16[16,16,384]{2,1,0:T(8,128)(2,1)} %couple.1), calls=%async_computation.2 | async-start | bytes 393216 | tf_op jit(solution)/shard_map/all_to_all | solution.py:301
  49.3 0.7 %copy-start.5 = (bf16[96,96]{1,0:T(8,128)(2,1)S(1)}, bf16[96,96]{1,0:T(8,128)(2,1)}, u32[]{:S(2)}) copy-start(bf16[96,96]{1,0:T(8,128)(2,1)} %out_map.1) | copy-start | bytes 55300
  49.3 0.7 %copy-start.6 = (bf16[96,96]{1,0:T(8,128)(2,1)S(1)}, bf16[96,96]{1,0:T(8,128)(2,1)}, u32[]{:S(2)}) copy-start(bf16[96,96]{1,0:T(8,128)(2,1)} %in_map.1) | copy-start | bytes 55300
  49.3 0.7 %copy-start.7 = (f32[16,96]{1,0:T(8,128)S(1)}, f32[16,96]{1,0:T(8,128)}, u32[]{:S(2)}) copy-start(f32[16,96]{1,0:T(8,128)} %tmat.1) | copy-start | bytes 18436
  49.3 0.7 %copy-start.9 = (s32[16]{0:T(128)S(1)}, s32[16]{0:T(128)}, u32[]{:S(2)}) copy-start(s32[16]{0:T(128)} %counts.1) | copy-start | bytes 196
  50.0 1.5 %copy-start.8 = (s32[16,32]{1,0:T(8,128)S(1)}, s32[16,32]{1,0:T(8,128)}, u32[]{:S(2)}) copy-start(s32[16,32]{1,0:T(8,128)} %nbr.1) | copy-start | bytes 6148

commit v3 on v2

--- a/solution.py
+++ b/solution.py
@@ -13,6 +13,7 @@
 NBG = 2
 LANES = 128
 HALF = 64
+UNROLL = 4
 
 
 def dot(a, b, ca=1, cb=0):
@@ -167,13 +168,18 @@
     )(counts, axial, rot, perm, permt, out_map, in_map, tmat)
 
 
-def near_kernel(nbr, low, own, high, scale, turn, out, planes, cand, diag, total):
+def near_kernel(nbr, low, own, high, scale, turn, out, sides, planes, cand, diag, total, sems):
     sd, slots = nbr.shape
+    copies = [pltpu.make_async_copy(src, sides.at[n], sems.at[n]) for n, src in enumerate((low, high))]
+    for copy in copies:
+        copy.start()
     lane = lax.broadcasted_iota(jnp.int32, (HALF, LANES), 1) < HALF
     diag[...] = jnp.zeros_like(diag)
     planes[...] = jnp.zeros_like(planes)
-    for c, part in enumerate((low, own, high)):
-        to_planes(part, planes, 0)
+    for c in (1, 0, 2):
+        if c != 1:
+            copies[c // 2].wait()
+        to_planes(own if c == 1 else sides[c // 2], planes, 0)
         for s in range(0, sd, 2):
             both = planes[s * HALF:(s + 2) * HALF, :].T
             top, bottom = both[:HALF], both[HALF:]
@@ -182,7 +188,7 @@
     total[...] = jnp.zeros_like(total)
     group = 4
 
-    def step(q, carry):
+    def pair(q, diag):
         k = 2 * q
         r = pl.multiple_of(q * 2 * LANES, 2 * LANES)
         diag[:LANES, :LANES] = turn[pl.ds(r, LANES), :]
@@ -204,9 +210,13 @@
                 scaled.append((turned[n * HALF:(n + 1) * HALF] * f).astype(BF16))
             rows = pl.ds(g * group * HALF, group * HALF)
             total[rows, :] += dot(jnp.concatenate(scaled, axis=0), back)
+
+    def step(m, carry):
+        for u in range(UNROLL):
+            pair(UNROLL * m + u, diag.at[u])
         return carry
 
-    lax.fori_loop(0, slots // 2, step, 0)
+    lax.fori_loop(0, slots // (2 * UNROLL), step, 0)
     for s in range(0, sd, 2):
         a = total[s * HALF:(s + 1) * HALF, :]
         b = total[(s + 1) * HALF:(s + 2) * HALF, :]
@@ -218,16 +228,19 @@
 def near_field(nbr, low, own, high, scale, turn):
     sd, _ = nbr.shape
     vmem = pl.BlockSpec(memory_space=pltpu.VMEM)
+    place = pl.BlockSpec(memory_space=pl.ANY)
     return pl.pallas_call(
         near_kernel,
         out_shape=jax.ShapeDtypeStruct((sd * HALF, LANES), F32),
-        in_specs=[pl.BlockSpec(memory_space=pltpu.SMEM)] + [vmem] * 5,
+        in_specs=[pl.BlockSpec(memory_space=pltpu.SMEM), place, vmem, place, vmem, vmem],
         out_specs=vmem,
         scratch_shapes=[
+            pltpu.VMEM((2, *own.shape), BF16),
             pltpu.VMEM((sd * HALF, LANES), F32),
             pltpu.VMEM((3 * sd, HALF, LANES), BF16),
-            pltpu.VMEM((2 * LANES, 2 * LANES), BF16),
+            pltpu.VMEM((UNROLL, 2 * LANES, 2 * LANES), BF16),
             pltpu.VMEM((sd * HALF, LANES), F32),
+            pltpu.SemaphoreType.DMA((2,)),
         ],
         compiler_params=params(),
         name="near",

time: 66.9 us -> 62.8 us (0.939)
  Pallas kernels: 18.6 us -> 14.5 us
    pallas_call x1, Pallas kernels: 13.5 us -> 9.39 us  [near_field(): pl.pallas_call(near_kernel, out_shape=jax.ShapeDtypeStruct((sd * HALF, LA...]
  transfers between devices with their start and end apart: 4 -> 4, of which waited for: 1 -> 1; matrix products, arithmetic and copies ran while one was open for 0% -> 0% of each run, Pallas kernels for 24% -> 19%
where the time goes in v3:
time: 62.8 us; the launch traced here: 62.4 us
  starting transfers between devices  22.4 us (36%)
  Pallas kernels  14.5 us (23%)
  blocking collectives  14.1 us (22%)
  waiting for transfers between devices  8.82 us (14%)
  local copies, waits for them, and re-layouts  1.63 us (3%)
  other arithmetic  0.76 us (1%)
    all_to_all x1, blocking collectives, shards(): got = lax.all_to_all(sent, 'grp', 0, 0, tiled=True)  14.1 us
    all_to_all x1, starting transfers between devices, shards(): every = lax.all_to_all(sums, 'cells', 0, 0, tiled=True)  10.2 us
    pallas_call x1, Pallas kernels, near_field(): pl.pallas_call(near_kernel, out_shape=jax.ShapeDtypeStruct((sd * HALF, LA...  9.39 us
    all_to_all x1, waiting for transfers between devices, shards(): every = lax.all_to_all(sums, 'cells', 0, 0, tiled=True)  8.81 us
    all_to_all x1, starting transfers between devices, shards(): mine = lax.all_to_all(local, 'grp', 0, 0, tiled=True)  6.76 us
    ppermute x1, starting transfers between devices, shards(): low = lax.ppermute(coeffs, 'cells', forward)  4.18 us
    unnamed x20, local copies, waits for them, and re-layouts  1.55 us
    pallas_call x1, Pallas kernels, tail(): pl.pallas_call(tail_kernel, out_shape=jax.ShapeDtypeStruct(coeffs.shape,...  1.49 us
  transfers between devices with their start and end apart: 4, of which 1 were waited for; matrix products, arithmetic and copies ran while one was open for 0% of the time, Pallas kernels for 19%

profile of v3, /device:TPU:1, one launch (start us, length us, event | category | flops | bytes accessed | tf_op | source)
XLA Modules:
  0.0 62.4 jit_solution(17861948908261472001)
XLA Ops:
  0.0 0.7 %convert_element_type.9 = bf16[16]{0:T(256)(128)(2,1)S(1)} convert(s32[16]{0:T(128)} %param.13) | non-fusion elementwise | flops 16 | bytes 96 | tf_op jit(solution)/shard_map/convert_element_type | solution.py:48
  0.7 0.1 broadcast_in_dim.5.boxes
  0.7 0.0 copy-start
  0.7 0.9 %copy-done = bf16[16,6144]{1,0:T(8,128)(2,1)S(1)} copy-done((bf16[16,6144]{1,0:T(8,128)(2,1)S(1)}, bf16[16,6144]{1,0:T(8,128)(2,1)}, u32[]{:S(2)}) %copy-start) | copy-done | bytes 196632
  1.7 14.1 %all_to_all.15.got = bf16[16,16,512]{2,1,0:T(8,128)(2,1)S(1)} all-to-all(bf16[16,16,512]{2,1,0:T(8,128)(2,1)S(1)} %pack.1), channel_id=1, replica_groups=mesh['cells'=16,'grp'=16] {'grp'}, dimensions={0} | all-to-all | bytes 524288 | tf_op jit(solution)/shard_map/all_to_all | solution.py:299
  15.8 0.0 copy-start.3
  15.8 1.0 %box_sums.1 = (bf16[16,32,384]{2,1,0:T(8,128)(2,1)}, bf16[256,32]{1,0:T(8,128)(2,1)S(1)}) custom-call(bf16[16,16,512]{2,1,0:T(8,128)(2,1)S(1)} %all_to_all.15.got), custom_call_target="tpu_custom_call" | custom-call | tf_op jit(solution)/shard_map/box_sums/pallas_call | solution.py:72
  16.8 0.0 copy-start.1
  16.8 10.2 %all-to-all-start.1 = ((bf16[16,32,384]{2,1,0:T(8,128)(2,1)}), bf16[16,32,384]{2,1,0:T(8,128)(2,1)S(1)}, u32[]{:S(2)}, u32[]{:S(2)}) async-start(bf16[16,32,384]{2,1,0:T(8,128)(2,1)} %get-tuple-element.13), calls=%async_computation.1 | async-start | bytes 786432 | tf_op jit(solution)/shard_map/all_to_all | solution.py:309
  27.0 0.0 copy-done.1
  27.0 4.2 %collective-permute-start = (bf16[16,6144]{1,0:T(8,128)(2,1)S(1)}, bf16[16,6144]{1,0:T(8,128)(2,1)S(1)}, u32[]{:S(2)}, u32[]{:S(2)}) collective-permute-start(bf16[16,6144]{1,0:T(8,128)(2,1)S(1)} %copy-done.1), channel_id=1, source_target_pairs={{0,16},{16,32},{32,48},{48,64},{64,80},{80,96},{96,112},{112,128},... | collective-permute-start | bytes 589832 | tf_op jit(solution)/shard_map/ppermute | solution.py:296
  31.2 1.3 %collective-permute-start.1 = (bf16[16,6144]{1,0:T(8,128)(2,1)S(1)}, bf16[16,6144]{1,0:T(8,128)(2,1)S(1)}, u32[]{:S(2)}, u32[]{:S(2)}) collective-permute-start(bf16[16,6144]{1,0:T(8,128)(2,1)S(1)} %copy-done.1), channel_id=1, source_target_pairs={{16,0},{32,16},{48,32},{64,48},{80,64},{96,80},{112,96},{128,112},... | collective-permute-start | bytes 589832 | tf_op jit(solution)/shard_map/ppermute | solution.py:297
  32.5 0.0 copy-done.3
  32.5 0.2 sphere_rows.1.rows
  32.7 0.0 copy-start.2
  32.7 8.8 %all-to-all-done.1.sums = bf16[16,32,384]{2,1,0:T(8,128)(2,1)S(1)} async-done(((bf16[16,32,384]{2,1,0:T(8,128)(2,1)}), bf16[16,32,384]{2,1,0:T(8,128)(2,1)S(1)}, u32[]{:S(2)}, u32[]{:S(2)}) %all-to-all-start.1) | async-done | bytes 393248 | tf_op jit(solution)/shard_map/all_to_all | solution.py:309
  41.5 1.0 %couple.1 = bf16[16,16,384]{2,1,0:T(8,128)(2,1)} custom-call(bf16[256,512]{1,0:T(8,128)(2,1)S(1)} %sphere_rows.1.rows, bf16[16,32,384]{2,1,0:T(8,128)(2,1)S(1)} %all-to-all-done.1.sums), custom_call_target="tpu_custom_call" | custom-call | tf_op jit(solution)/shard_map/couple/pallas_call | solution.py:115
  42.5 0.0 copy-start.4
  42.5 6.8 %all-to-all-start.2 = ((bf16[16,16,384]{2,1,0:T(8,128)(2,1)}), bf16[16,16,384]{2,1,0:T(8,128)(2,1)S(1)}, u32[]{:S(2)}, u32[]{:S(2)}) async-start(bf16[16,16,384]{2,1,0:T(8,128)(2,1)} %couple.1), calls=%async_computation.2 | async-start | bytes 393216 | tf_op jit(solution)/shard_map/all_to_all | solution.py:314
  49.3 0.0 copy-start.5
  49.3 0.0 copy-start.6
  49.3 0.0 copy-start.7
  49.3 0.0 copy-start.9
  49.3 0.1 fusion.1.perm
  49.4 0.0 copy-done.2
  49.4 0.0 copy-done.4
  49.4 0.6 copy-done.5
  50.0 0.0 copy-done.6
  50.0 0.0 copy-done.7
  50.0 0.0 copy-done.9
  50.0 0.0 copy-start.8
  50.0 1.4 %prepare.1 = (bf16[4096,128]{1,0:T(8,128)(2,1)S(1)}, f32[512,128]{1,0:T(8,128)S(1)}, bf16[256,128]{1,0:T(8,128)(2,1)S(1)}, f32[16,24,128]{2,1,0:T(8,128)S(1)}, f32[16,24,128]{2,1,0:T(8,128)S(1)}) custom-call(s32[16]{0:T(128)S(1)} %copy-done.9, bf16[16,32,96]{2,1,0:T(8,128)(2,1)S(1)} %copy-done.4, bf16[32,96,96]{2,1,0:T(8,128)(2,1)S(1)} %copy-done.2, ...), custom_call_target="tpu_custom_call" | custom-call | tf_op jit(solution)/shard_map/prepare/pallas_call | solution.py:155
  51.5 0.0 collective-permute-done.low
  51.5 0.0 collective-permute-done.1.high
  51.5 0.0 copy-done.8
  51.5 9.4 %near.1 = f32[1024,128]{1,0:T(8,128)S(1)} custom-call(s32[16,32]{1,0:T(8,128)S(1)} %copy-done.8, bf16[16,6144]{1,0:T(8,128)(2,1)S(1)} %collective-permute-done.low, bf16[16,6144]{1,0:T(8,128)(2,1)S(1)} %copy-done.1, bf16[16,6144]{1,0:T(8,128)(2,1)S(1)} %collective-permute-done.1.high, f32[512,128]{1,0:T(8,128)S(1)} %get-tuple-element.14.scale, ...), custom_call_target="tpu_custom_call" | custom-call | tf_op jit(solution)/shard_map/near/pallas_call | solution.py:232
  60.9 0.0 all-to-all-done.2.got
  60.9 1.5 %tail.1 = bf16[16,6144]{1,0:T(8,128)(2,1)} custom-call(bf16[16,16,384]{2,1,0:T(8,128)(2,1)S(1)} %all-to-all-done.2.got, f32[1024,128]{1,0:T(8,128)S(1)} %near.1, bf16[16,6144]{1,0:T(8,128)(2,1)S(1)} %copy-done.1, f32[16,24,128]{2,1,0:T(8,128)S(1)} %get-tuple-element.16.tmat_re, f32[16,24,128]{2,1,0:T(8,128)S(1)} %get-tuple-element.17.tmat_im, ...), custom_call_target="tpu_custom_call" | custom-call | tf_op jit(solution)/shard_map/tail/pallas_call | solution.py:279
  (3 shorter events, 0.0 us)
Async XLA Ops:
  0.7 0.9 %copy-start = (bf16[16,6144]{1,0:T(8,128)(2,1)S(1)}, bf16[16,6144]{1,0:T(8,128)(2,1)}, u32[]{:S(2)}) copy-start(bf16[16,6144]{1,0:T(8,128)(2,1)} %x.3) | copy-start | bytes 589828
  15.8 16.6 %copy-start.3 = (bf16[512,512]{1,0:T(8,128)(2,1)S(1)}, bf16[512,512]{1,0:T(8,128)(2,1)}, u32[]{:S(2)}) copy-start(bf16[512,512]{1,0:T(8,128)(2,1)} %coupling.1) | copy-start | bytes 1572868
  16.8 10.2 %copy-start.1 = (bf16[16,6144]{1,0:T(8,128)(2,1)S(1)}, bf16[16,6144]{1,0:T(8,128)(2,1)}, u32[]{:S(2)}) copy-start(bf16[16,6144]{1,0:T(8,128)(2,1)} %x.3) | copy-start | bytes 589828
  16.8 24.7 %all-to-all-start.1 = ((bf16[16,32,384]{2,1,0:T(8,128)(2,1)}), bf16[16,32,384]{2,1,0:T(8,128)(2,1)S(1)}, u32[]{:S(2)}, u32[]{:S(2)}) async-start(bf16[16,32,384]{2,1,0:T(8,128)(2,1)} %get-tuple-element.13), calls=%async_computation.1 | async-start | bytes 786432 | tf_op jit(solution)/shard_map/all_to_all | solution.py:309
  27.0 24.5 %collective-permute-start = (bf16[16,6144]{1,0:T(8,128)(2,1)S(1)}, bf16[16,6144]{1,0:T(8,128)(2,1)S(1)}, u32[]{:S(2)}, u32[]{:S(2)}) collective-permute-start(bf16[16,6144]{1,0:T(8,128)(2,1)S(1)} %copy-done.1), channel_id=1, source_target_pairs={{0,16},{16,32},{32,48},{48,64},{64,80},{80,96},{96,112},{112,128},... | collective-permute-start | bytes 589832 | tf_op jit(solution)/shard_map/ppermute | solution.py:296
  31.2 20.3 %collective-permute-start.1 = (bf16[16,6144]{1,0:T(8,128)(2,1)S(1)}, bf16[16,6144]{1,0:T(8,128)(2,1)S(1)}, u32[]{:S(2)}, u32[]{:S(2)}) collective-permute-start(bf16[16,6144]{1,0:T(8,128)(2,1)S(1)} %copy-done.1), channel_id=1, source_target_pairs={{16,0},{32,16},{48,32},{64,48},{80,64},{96,80},{112,96},{128,112},... | collective-permute-start | bytes 589832 | tf_op jit(solution)/shard_map/ppermute | solution.py:297
  32.7 16.7 %copy-start.2 = (bf16[32,96,96]{2,1,0:T(8,128)(2,1)S(1)}, bf16[32,96,96]{2,1,0:T(8,128)(2,1)}, u32[]{:S(2)}) copy-start(bf16[32,96,96]{2,1,0:T(8,128)(2,1)} %rot.1) | copy-start | bytes 1769476
  42.5 6.9 %copy-start.4 = (bf16[16,32,96]{2,1,0:T(8,128)(2,1)S(1)}, bf16[16,32,96]{2,1,0:T(8,128)(2,1)}, u32[]{:S(2)}) copy-start(bf16[16,32,96]{2,1,0:T(8,128)(2,1)} %axial.1) | copy-start | bytes 294916
  42.5 18.4 %all-to-all-start.2 = ((bf16[16,16,384]{2,1,0:T(8,128)(2,1)}), bf16[16,16,384]{2,1,0:T(8,128)(2,1)S(1)}, u32[]{:S(2)}, u32[]{:S(2)}) async-start(bf16[16,16,384]{2,1,0:T(8,128)(2,1)} %couple.1), calls=%async_computation.2 | async-start | bytes 393216 | tf_op jit(solution)/shard_map/all_to_all | solution.py:314
  49.3 0.7 %copy-start.5 = (bf16[96,96]{1,0:T(8,128)(2,1)S(1)}, bf16[96,96]{1,0:T(8,128)(2,1)}, u32[]{:S(2)}) copy-start(bf16[96,96]{1,0:T(8,128)(2,1)} %out_map.1) | copy-start | bytes 55300
  49.3 0.7 %copy-start.6 = (bf16[96,96]{1,0:T(8,128)(2,1)S(1)}, bf16[96,96]{1,0:T(8,128)(2,1)}, u32[]{:S(2)}) copy-start(bf16[96,96]{1,0:T(8,128)(2,1)} %in_map.1) | copy-start | bytes 55300
  49.3 0.7 %copy-start.7 = (f32[16,96]{1,0:T(8,128)S(1)}, f32[16,96]{1,0:T(8,128)}, u32[]{:S(2)}) copy-start(f32[16,96]{1,0:T(8,128)} %tmat.1) | copy-start | bytes 18436
  49.3 0.7 %copy-start.9 = (s32[16]{0:T(128)S(1)}, s32[16]{0:T(128)}, u32[]{:S(2)}) copy-start(s32[16]{0:T(128)} %counts.1) | copy-start | bytes 196
  50.0 1.5 %copy-start.8 = (s32[16,32]{1,0:T(8,128)S(1)}, s32[16,32]{1,0:T(8,128)}, u32[]{:S(2)}) copy-start(s32[16,32]{1,0:T(8,128)} %nbr.1) | copy-start | bytes 6148

commit v4 on v3

--- a/solution.py
+++ b/solution.py
@@ -168,23 +168,24 @@
     )(counts, axial, rot, perm, permt, out_map, in_map, tmat)
 
 
-def near_kernel(nbr, low, own, high, scale, turn, out, sides, planes, cand, diag, total, sems):
+def near_kernel(nbr, column, side_a, own, side_b, scale, turn, out, sides, planes, cand, diag, total, sems):
     sd, slots = nbr.shape
-    copies = [pltpu.make_async_copy(src, sides.at[n], sems.at[n]) for n, src in enumerate((low, high))]
+    copies = [pltpu.make_async_copy(src, sides.at[n], sems.at[n]) for n, src in enumerate((side_a, side_b))]
     for copy in copies:
         copy.start()
     lane = lax.broadcasted_iota(jnp.int32, (HALF, LANES), 1) < HALF
     diag[...] = jnp.zeros_like(diag)
     planes[...] = jnp.zeros_like(planes)
-    for c in (1, 0, 2):
+    odd = column[0] % 2
+    for c, base in ((1, sd), (0, 2 * sd * (1 - odd)), (2, 2 * sd * odd)):
         if c != 1:
             copies[c // 2].wait()
         to_planes(own if c == 1 else sides[c // 2], planes, 0)
         for s in range(0, sd, 2):
             both = planes[s * HALF:(s + 2) * HALF, :].T
             top, bottom = both[:HALF], both[HALF:]
-            cand[c * sd + s] = jnp.where(lane, top, swap_halves(bottom)).astype(BF16)
-            cand[c * sd + s + 1] = jnp.where(lane, swap_halves(top), bottom).astype(BF16)
+            cand[base + s] = jnp.where(lane, top, swap_halves(bottom)).astype(BF16)
+            cand[base + s + 1] = jnp.where(lane, swap_halves(top), bottom).astype(BF16)
     total[...] = jnp.zeros_like(total)
     group = 4
 
@@ -225,14 +226,14 @@
         out[s * HALF:(s + 2) * HALF, :] = jnp.concatenate([top, bottom], axis=0).T
 
 
-def near_field(nbr, low, own, high, scale, turn):
+def near_field(nbr, column, side_a, own, side_b, scale, turn):
     sd, _ = nbr.shape
     vmem = pl.BlockSpec(memory_space=pltpu.VMEM)
     place = pl.BlockSpec(memory_space=pl.ANY)
     return pl.pallas_call(
         near_kernel,
         out_shape=jax.ShapeDtypeStruct((sd * HALF, LANES), F32),
-        in_specs=[pl.BlockSpec(memory_space=pltpu.SMEM), place, vmem, place, vmem, vmem],
+        in_specs=[pl.BlockSpec(memory_space=pltpu.SMEM)] * 2 + [place, vmem, place, vmem, vmem],
         out_specs=vmem,
         scratch_shapes=[
             pltpu.VMEM((2, *own.shape), BF16),
@@ -244,7 +245,7 @@
         ],
         compiler_params=params(),
         name="near",
-    )(nbr, low, own, high, scale, turn)
+    )(nbr, column, side_a, own, side_b, scale, turn)
 
 
 def tail_kernel(got, near, x, tmat_re, tmat_im, maps, out, planes):
@@ -291,10 +292,11 @@
     ngrp = lax.axis_size("grp")
     ncell = lax.axis_size("cells")
     nbc = NBG * ngrp
-    forward = [(i, i + 1) for i in range(ncell - 1)]
-    backward = [(b, a) for a, b in forward]
-    low = lax.ppermute(coeffs, "cells", forward)
-    high = lax.ppermute(coeffs, "cells", backward)
+    first = [p for i in range(0, ncell - 1, 2) for p in ((i, i + 1), (i + 1, i))]
+    second = [p for i in range(1, ncell - 1, 2) for p in ((i, i + 1), (i + 1, i))]
+    column = lax.axis_index("cells").astype(jnp.int32)[None]
+    near_a = lax.ppermute(coeffs, "cells", first)
+    near_b = lax.ppermute(coeffs, "cells", second)
     sent = pack(coeffs, boxes, ngrp)
     got = lax.all_to_all(sent, "grp", 0, 0, tiled=True)
     spot = jnp.arange(width, dtype=jnp.int32)
@@ -307,9 +309,8 @@
     )
     sums, onehot = box_sums(got, nbc, ncell)
     every = lax.all_to_all(sums, "cells", 0, 0, tiled=True)
-    column = lax.axis_index("cells").astype(jnp.int32)[None]
     rows = sphere_rows(column, onehot, coupling)
-    near = near_field(neighbours, low, coeffs, high, scale, turn)
+    near = near_field(neighbours, column, near_a, coeffs, near_b, scale, turn)
     local = couple(rows, every, ngrp, sd)
     mine = lax.all_to_all(local, "grp", 0, 0, tiled=True)
     return tail(mine, near, coeffs, tre, tim, maps)

time: 62.8 us -> 62.8 us (level)
  starting transfers between devices: 22.4 us -> 19.9 us
  waiting for transfers between devices: 8.82 us -> 11.3 us
    all_to_all x1, waiting for transfers between devices: 8.81 us -> 11.3 us  [shards(): every = lax.all_to_all(sums, 'cells', 0, 0, tiled=True)]
    ppermute x2, starting transfers between devices: 5.47 us -> 3.01 us  [the longest x1 2.35 us: shards(): near_a = lax.ppermute(coeffs, 'cells', first)]
where the time goes in v4:
time: 62.8 us; the launch traced here: 62.4 us
  starting transfers between devices  19.9 us (32%)
  Pallas kernels  14.5 us (23%)
  blocking collectives  14.1 us (22%)
  waiting for transfers between devices  11.3 us (18%)
  local copies, waits for them, and re-layouts  1.63 us (3%)
  other arithmetic  0.76 us (1%)
    all_to_all x1, blocking collectives, shards(): got = lax.all_to_all(sent, 'grp', 0, 0, tiled=True)  14.1 us
    all_to_all x1, waiting for transfers between devices, shards(): every = lax.all_to_all(sums, 'cells', 0, 0, tiled=True)  11.3 us
    all_to_all x1, starting transfers between devices, shards(): every = lax.all_to_all(sums, 'cells', 0, 0, tiled=True)  10.2 us
    pallas_call x1, Pallas kernels, near_field(): pl.pallas_call(near_kernel, out_shape=jax.ShapeDtypeStruct((sd * HALF, LA...  9.4 us
    all_to_all x1, starting transfers between devices, shards(): mine = lax.all_to_all(local, 'grp', 0, 0, tiled=True)  6.72 us
    ppermute x1, starting transfers between devices, shards(): near_a = lax.ppermute(coeffs, 'cells', first)  2.35 us
    unnamed x20, local copies, waits for them, and re-layouts  1.55 us
    pallas_call x1, Pallas kernels, tail(): pl.pallas_call(tail_kernel, out_shape=jax.ShapeDtypeStruct(coeffs.shape,...  1.49 us
  transfers between devices with their start and end apart: 4, of which 1 were waited for; matrix products, arithmetic and copies ran while one was open for 0% of the time, Pallas kernels for 19%

profile of v4, /device:TPU:1, one launch (start us, length us, event | category | flops | bytes accessed | tf_op | source)
XLA Modules:
  0.0 62.4 jit_solution(16357080252036897842)
XLA Ops:
  0.0 0.7 %convert_element_type.9 = bf16[16]{0:T(256)(128)(2,1)S(1)} convert(s32[16]{0:T(128)} %param.13) | non-fusion elementwise | flops 16 | bytes 96 | tf_op jit(solution)/shard_map/convert_element_type | solution.py:48
  0.7 0.1 broadcast_in_dim.5.boxes
  0.7 0.0 copy-start
  0.7 0.9 %copy-done = bf16[16,6144]{1,0:T(8,128)(2,1)S(1)} copy-done((bf16[16,6144]{1,0:T(8,128)(2,1)S(1)}, bf16[16,6144]{1,0:T(8,128)(2,1)}, u32[]{:S(2)}) %copy-start) | copy-done | bytes 196632
  1.7 14.1 %all_to_all.15.got = bf16[16,16,512]{2,1,0:T(8,128)(2,1)S(1)} all-to-all(bf16[16,16,512]{2,1,0:T(8,128)(2,1)S(1)} %pack.1), channel_id=1, replica_groups=mesh['cells'=16,'grp'=16] {'grp'}, dimensions={0} | all-to-all | bytes 524288 | tf_op jit(solution)/shard_map/all_to_all | solution.py:301
  15.8 0.0 copy-start.3
  15.8 1.0 %box_sums.1 = (bf16[16,32,384]{2,1,0:T(8,128)(2,1)}, bf16[256,32]{1,0:T(8,128)(2,1)S(1)}) custom-call(bf16[16,16,512]{2,1,0:T(8,128)(2,1)S(1)} %all_to_all.15.got), custom_call_target="tpu_custom_call" | custom-call | tf_op jit(solution)/shard_map/box_sums/pallas_call | solution.py:72
  16.8 0.0 copy-start.1
  16.8 10.2 %all-to-all-start.1 = ((bf16[16,32,384]{2,1,0:T(8,128)(2,1)}), bf16[16,32,384]{2,1,0:T(8,128)(2,1)S(1)}, u32[]{:S(2)}, u32[]{:S(2)}) async-start(bf16[16,32,384]{2,1,0:T(8,128)(2,1)} %get-tuple-element.13), calls=%async_computation.1 | async-start | bytes 786432 | tf_op jit(solution)/shard_map/all_to_all | solution.py:311
  27.0 0.0 copy-done.1
  27.0 2.3 %collective-permute-start = (bf16[16,6144]{1,0:T(8,128)(2,1)S(1)}, bf16[16,6144]{1,0:T(8,128)(2,1)S(1)}, u32[]{:S(2)}, u32[]{:S(2)}) collective-permute-start(bf16[16,6144]{1,0:T(8,128)(2,1)S(1)} %copy-done.1), channel_id=1, source_target_pairs={{0,16},{16,0},{32,48},{48,32},{64,80},{80,64},{96,112},{112,96},{1... | collective-permute-start | bytes 589832 | tf_op jit(solution)/shard_map/ppermute | solution.py:298
  29.3 0.7 %collective-permute-start.1 = (bf16[16,6144]{1,0:T(8,128)(2,1)S(1)}, bf16[16,6144]{1,0:T(8,128)(2,1)S(1)}, u32[]{:S(2)}, u32[]{:S(2)}) collective-permute-start(bf16[16,6144]{1,0:T(8,128)(2,1)S(1)} %copy-done.1), channel_id=1, source_target_pairs={{16,32},{32,16},{48,64},{64,48},{80,96},{96,80},{112,128},{128,112... | collective-permute-start | bytes 589832 | tf_op jit(solution)/shard_map/ppermute | solution.py:299
  30.0 0.0 copy-done.3
  30.0 0.2 sphere_rows.1.rows
  30.2 0.0 copy-start.2
  30.2 11.3 %all-to-all-done.1.sums = bf16[16,32,384]{2,1,0:T(8,128)(2,1)S(1)} async-done(((bf16[16,32,384]{2,1,0:T(8,128)(2,1)}), bf16[16,32,384]{2,1,0:T(8,128)(2,1)S(1)}, u32[]{:S(2)}, u32[]{:S(2)}) %all-to-all-start.1) | async-done | bytes 393248 | tf_op jit(solution)/shard_map/all_to_all | solution.py:311
  41.6 1.0 %couple.1 = bf16[16,16,384]{2,1,0:T(8,128)(2,1)} custom-call(bf16[256,512]{1,0:T(8,128)(2,1)S(1)} %sphere_rows.1.rows, bf16[16,32,384]{2,1,0:T(8,128)(2,1)S(1)} %all-to-all-done.1.sums), custom_call_target="tpu_custom_call" | custom-call | tf_op jit(solution)/shard_map/couple/pallas_call | solution.py:115
  42.5 0.0 copy-start.4
  42.5 6.7 %all-to-all-start.2 = ((bf16[16,16,384]{2,1,0:T(8,128)(2,1)}), bf16[16,16,384]{2,1,0:T(8,128)(2,1)S(1)}, u32[]{:S(2)}, u32[]{:S(2)}) async-start(bf16[16,16,384]{2,1,0:T(8,128)(2,1)} %couple.1), calls=%async_computation.2 | async-start | bytes 393216 | tf_op jit(solution)/shard_map/all_to_all | solution.py:315
  49.3 0.0 copy-start.5
  49.3 0.0 copy-start.6
  49.3 0.0 copy-start.7
  49.3 0.0 copy-start.9
  49.3 0.1 fusion.1.perm
  49.4 0.0 copy-done.2
  49.4 0.0 copy-done.4
  49.4 0.6 copy-done.5
  50.0 0.0 copy-done.6
  50.0 0.0 copy-done.7
  50.0 0.0 copy-done.9
  50.0 0.0 copy-start.8
  50.0 1.4 %prepare.1 = (bf16[4096,128]{1,0:T(8,128)(2,1)S(1)}, f32[512,128]{1,0:T(8,128)S(1)}, bf16[256,128]{1,0:T(8,128)(2,1)S(1)}, f32[16,24,128]{2,1,0:T(8,128)S(1)}, f32[16,24,128]{2,1,0:T(8,128)S(1)}) custom-call(s32[16]{0:T(128)S(1)} %copy-done.9, bf16[16,32,96]{2,1,0:T(8,128)(2,1)S(1)} %copy-done.4, bf16[32,96,96]{2,1,0:T(8,128)(2,1)S(1)} %copy-done.2, ...), custom_call_target="tpu_custom_call" | custom-call | tf_op jit(solution)/shard_map/prepare/pallas_call | solution.py:155
  51.5 0.0 collective-permute-done.side_a
  51.5 0.0 collective-permute-done.1.side_b
  51.5 0.0 copy-done.8
  51.5 9.4 %near.1 = f32[1024,128]{1,0:T(8,128)S(1)} custom-call(s32[16,32]{1,0:T(8,128)S(1)} %copy-done.8, s32[1]{0:T(128)} %bitcast.column, bf16[16,6144]{1,0:T(8,128)(2,1)S(1)} %collective-permute-done.side_a, bf16[16,6144]{1,0:T(8,128)(2,1)S(1)} %copy-done.1, bf16[16,6144]{1,0:T(8,128)(2,1)S(1)} %collective-permute-done.1.side_b, ...), custom_call_target="tpu_custom_call" | custom-call | tf_op jit(solution)/shard_map/near/pallas_call | solution.py:233
  60.9 0.0 all-to-all-done.2.got
  60.9 1.5 %tail.1 = bf16[16,6144]{1,0:T(8,128)(2,1)} custom-call(bf16[16,16,384]{2,1,0:T(8,128)(2,1)S(1)} %all-to-all-done.2.got, f32[1024,128]{1,0:T(8,128)S(1)} %near.1, bf16[16,6144]{1,0:T(8,128)(2,1)S(1)} %copy-done.1, f32[16,24,128]{2,1,0:T(8,128)S(1)} %get-tuple-element.16.tmat_re, f32[16,24,128]{2,1,0:T(8,128)S(1)} %get-tuple-element.17.tmat_im, ...), custom_call_target="tpu_custom_call" | custom-call | tf_op jit(solution)/shard_map/tail/pallas_call | solution.py:280
  (3 shorter events, 0.0 us)
Async XLA Ops:
  0.7 0.9 %copy-start = (bf16[16,6144]{1,0:T(8,128)(2,1)S(1)}, bf16[16,6144]{1,0:T(8,128)(2,1)}, u32[]{:S(2)}) copy-start(bf16[16,6144]{1,0:T(8,128)(2,1)} %x.3) | copy-start | bytes 589828
  15.8 14.2 %copy-start.3 = (bf16[512,512]{1,0:T(8,128)(2,1)S(1)}, bf16[512,512]{1,0:T(8,128)(2,1)}, u32[]{:S(2)}) copy-start(bf16[512,512]{1,0:T(8,128)(2,1)} %coupling.1) | copy-start | bytes 1572868
  16.8 10.2 %copy-start.1 = (bf16[16,6144]{1,0:T(8,128)(2,1)S(1)}, bf16[16,6144]{1,0:T(8,128)(2,1)}, u32[]{:S(2)}) copy-start(bf16[16,6144]{1,0:T(8,128)(2,1)} %x.3) | copy-start | bytes 589828
  16.8 24.7 %all-to-all-start.1 = ((bf16[16,32,384]{2,1,0:T(8,128)(2,1)}), bf16[16,32,384]{2,1,0:T(8,128)(2,1)S(1)}, u32[]{:S(2)}, u32[]{:S(2)}) async-start(bf16[16,32,384]{2,1,0:T(8,128)(2,1)} %get-tuple-element.13), calls=%async_computation.1 | async-start | bytes 786432 | tf_op jit(solution)/shard_map/all_to_all | solution.py:311
  27.0 24.5 %collective-permute-start = (bf16[16,6144]{1,0:T(8,128)(2,1)S(1)}, bf16[16,6144]{1,0:T(8,128)(2,1)S(1)}, u32[]{:S(2)}, u32[]{:S(2)}) collective-permute-start(bf16[16,6144]{1,0:T(8,128)(2,1)S(1)} %copy-done.1), channel_id=1, source_target_pairs={{0,16},{16,0},{32,48},{48,32},{64,80},{80,64},{96,112},{112,96},{1... | collective-permute-start | bytes 589832 | tf_op jit(solution)/shard_map/ppermute | solution.py:298
  29.3 22.1 %collective-permute-start.1 = (bf16[16,6144]{1,0:T(8,128)(2,1)S(1)}, bf16[16,6144]{1,0:T(8,128)(2,1)S(1)}, u32[]{:S(2)}, u32[]{:S(2)}) collective-permute-start(bf16[16,6144]{1,0:T(8,128)(2,1)S(1)} %copy-done.1), channel_id=1, source_target_pairs={{16,32},{32,16},{48,64},{64,48},{80,96},{96,80},{112,128},{128,112... | collective-permute-start | bytes 589832 | tf_op jit(solution)/shard_map/ppermute | solution.py:299
  30.2 19.2 %copy-start.2 = (bf16[32,96,96]{2,1,0:T(8,128)(2,1)S(1)}, bf16[32,96,96]{2,1,0:T(8,128)(2,1)}, u32[]{:S(2)}) copy-start(bf16[32,96,96]{2,1,0:T(8,128)(2,1)} %rot.1) | copy-start | bytes 1769476
  42.5 6.9 %copy-start.4 = (bf16[16,32,96]{2,1,0:T(8,128)(2,1)S(1)}, bf16[16,32,96]{2,1,0:T(8,128)(2,1)}, u32[]{:S(2)}) copy-start(bf16[16,32,96]{2,1,0:T(8,128)(2,1)} %axial.1) | copy-start | bytes 294916
  42.5 18.4 %all-to-all-start.2 = ((bf16[16,16,384]{2,1,0:T(8,128)(2,1)}), bf16[16,16,384]{2,1,0:T(8,128)(2,1)S(1)}, u32[]{:S(2)}, u32[]{:S(2)}) async-start(bf16[16,16,384]{2,1,0:T(8,128)(2,1)} %couple.1), calls=%async_computation.2 | async-start | bytes 393216 | tf_op jit(solution)/shard_map/all_to_all | solution.py:315
  49.3 0.7 %copy-start.5 = (bf16[96,96]{1,0:T(8,128)(2,1)S(1)}, bf16[96,96]{1,0:T(8,128)(2,1)}, u32[]{:S(2)}) copy-start(bf16[96,96]{1,0:T(8,128)(2,1)} %out_map.1) | copy-start | bytes 55300
  49.3 0.7 %copy-start.6 = (bf16[96,96]{1,0:T(8,128)(2,1)S(1)}, bf16[96,96]{1,0:T(8,128)(2,1)}, u32[]{:S(2)}) copy-start(bf16[96,96]{1,0:T(8,128)(2,1)} %in_map.1) | copy-start | bytes 55300
  49.3 0.7 %copy-start.7 = (f32[16,96]{1,0:T(8,128)S(1)}, f32[16,96]{1,0:T(8,128)}, u32[]{:S(2)}) copy-start(f32[16,96]{1,0:T(8,128)} %tmat.1) | copy-start | bytes 18436
  49.3 0.7 %copy-start.9 = (s32[16]{0:T(128)S(1)}, s32[16]{0:T(128)}, u32[]{:S(2)}) copy-start(s32[16]{0:T(128)} %counts.1) | copy-start | bytes 196
  50.0 1.5 %copy-start.8 = (s32[16,32]{1,0:T(8,128)S(1)}, s32[16,32]{1,0:T(8,128)}, u32[]{:S(2)}) copy-start(s32[16,32]{1,0:T(8,128)} %nbr.1) | copy-start | bytes 6148

commit v5 on v4

--- a/solution.py
+++ b/solution.py
@@ -13,7 +13,7 @@
 NBG = 2
 LANES = 128
 HALF = 64
-UNROLL = 4
+UNROLL = 8
 
 
 def dot(a, b, ca=1, cb=0):
@@ -34,10 +34,14 @@
     return pltpu.roll(a, HALF, 1)
 
 
-def pack_kernel(x, boxes, out):
-    ngrp = out.shape[0]
-    feat = x.shape[1] // ngrp
-    tag = boxes[...]
+def pack_kernel(boxes, x, out):
+    ngrp, sd, wide = out.shape
+    feat = wide - LANES
+    row = lax.broadcasted_iota(jnp.int32, (sd, LANES), 0)
+    mark = jnp.zeros((sd, LANES), F32)
+    for s in range(sd):
+        mark = jnp.where(row == s, boxes[s].astype(F32), mark)
+    tag = mark.astype(BF16)
     for g in range(ngrp):
         out[g, :, :feat] = x[:, g * feat:(g + 1) * feat]
         out[g, :, feat:] = tag
@@ -45,13 +49,15 @@
 
 def pack(coeffs, boxes, ngrp):
     sd, width = coeffs.shape
-    tag = jnp.broadcast_to(boxes.astype(BF16)[:, None], (sd, LANES))
+    vmem = pl.BlockSpec(memory_space=pltpu.VMEM)
     return pl.pallas_call(
         pack_kernel,
         out_shape=jax.ShapeDtypeStruct((ngrp, sd, width // ngrp + LANES), BF16),
-        compiler_params=params(),
+        in_specs=[pl.BlockSpec(memory_space=pltpu.SMEM), vmem],
+        out_specs=vmem,
+        compiler_params=pltpu.CompilerParams(vmem_limit_bytes=62 * 1024 * 1024),
         name="pack",
-    )(coeffs, tag)
+    )(boxes, coeffs)
 
 
 def sums_kernel(got, out, onehot, *, nbc):

time: 62.8 us -> 62.1 us (0.989)
  local copies, waits for them, and re-layouts: 1.63 us -> 0.62 us
  Pallas kernels: 14.5 us -> 15.2 us
  other arithmetic: 0.76 us -> 0.1 us
    pallas_call x1, Pallas kernels: 0.03 us -> 1.66 us  [pack(): pl.pallas_call(pack_kernel, out_shape=jax.ShapeDtypeStruct((ngrp, sd, wid...]
    unnamed x20 -> x18, local copies, waits for them, and re-layouts: 1.55 us -> 0.62 us
    pallas_call x1, Pallas kernels: 9.4 us -> 8.48 us  [near_field(): pl.pallas_call(near_kernel, out_shape=jax.ShapeDtypeStruct((sd * HALF, LA...]
    convert_element_type x1 -> x0, other arithmetic: 0.66 us -> none  [pack(): tag = jnp.broadcast_to(boxes.astype(BF16)[:, None], (sd, LANES))]
  transfers between devices with their start and end apart: 4 -> 4, of which waited for: 1 -> 1; matrix products, arithmetic and copies ran while one was open for 0% -> 0% of each run, Pallas kernels for 19% -> 18%
where the time goes in v5:
time: 62.1 us; the launch traced here: 61.6 us
  starting transfers between devices  19.9 us (32%)
  Pallas kernels  15.2 us (24%)
  blocking collectives  14.3 us (23%)
  waiting for transfers between devices  11.3 us (18%)
    all_to_all x1, blocking collectives, shards(): got = lax.all_to_all(sent, 'grp', 0, 0, tiled=True)  14.3 us
    all_to_all x1, waiting for transfers between devices, shards(): every = lax.all_to_all(sums, 'cells', 0, 0, tiled=True)  11.3 us
    all_to_all x1, starting transfers between devices, shards(): every = lax.all_to_all(sums, 'cells', 0, 0, tiled=True)  10.2 us
    pallas_call x1, Pallas kernels, near_field(): pl.pallas_call(near_kernel, out_shape=jax.ShapeDtypeStruct((sd * HALF, LA...  8.48 us
    all_to_all x1, starting transfers between devices, shards(): mine = lax.all_to_all(local, 'grp', 0, 0, tiled=True)  6.72 us
    ppermute x1, starting transfers between devices, shards(): near_a = lax.ppermute(coeffs, 'cells', first)  2.35 us
    pallas_call x1, Pallas kernels, pack(): pl.pallas_call(pack_kernel, out_shape=jax.ShapeDtypeStruct((ngrp, sd, wid...  1.66 us
    pallas_call x1, Pallas kernels, tail(): pl.pallas_call(tail_kernel, out_shape=jax.ShapeDtypeStruct(coeffs.shape,...  1.49 us
  transfers between devices with their start and end apart: 4, of which 1 were waited for; matrix products, arithmetic and copies ran while one was open for 0% of the time, Pallas kernels for 18%

profile of v5, /device:TPU:1, one launch (start us, length us, event | category | flops | bytes accessed | tf_op | source)
XLA Modules:
  0.0 61.6 jit_solution(4826409694829615724)
XLA Ops:
  0.0 1.7 %pack.1 = bf16[16,16,512]{2,1,0:T(8,128)(2,1)} custom-call(s32[16]{0:T(128)} %boxes.1, bf16[16,6144]{1,0:T(8,128)(2,1)} %x.3), custom_call_target="tpu_custom_call" | custom-call | tf_op jit(solution)/shard_map/pack/pallas_call | solution.py:53
  1.7 14.3 %all_to_all.15.got = bf16[16,16,512]{2,1,0:T(8,128)(2,1)S(1)} all-to-all(bf16[16,16,512]{2,1,0:T(8,128)(2,1)} %pack.1), channel_id=1, replica_groups=mesh['cells'=16,'grp'=16] {'grp'}, dimensions={0} | all-to-all | bytes 524288 | tf_op jit(solution)/shard_map/all_to_all | solution.py:307
  16.0 0.0 copy-start.2
  16.0 1.0 %box_sums.1 = (bf16[16,32,384]{2,1,0:T(8,128)(2,1)}, bf16[256,32]{1,0:T(8,128)(2,1)S(1)}) custom-call(bf16[16,16,512]{2,1,0:T(8,128)(2,1)S(1)} %all_to_all.15.got), custom_call_target="tpu_custom_call" | custom-call | tf_op jit(solution)/shard_map/box_sums/pallas_call | solution.py:78
  17.0 0.0 copy-start
  17.0 10.2 %all-to-all-start.1 = ((bf16[16,32,384]{2,1,0:T(8,128)(2,1)}), bf16[16,32,384]{2,1,0:T(8,128)(2,1)S(1)}, u32[]{:S(2)}, u32[]{:S(2)}) async-start(bf16[16,32,384]{2,1,0:T(8,128)(2,1)} %get-tuple-element.13), calls=%async_computation.1 | async-start | bytes 786432 | tf_op jit(solution)/shard_map/all_to_all | solution.py:317
  27.1 0.0 copy-done
  27.2 2.3 %collective-permute-start = (bf16[16,6144]{1,0:T(8,128)(2,1)S(1)}, bf16[16,6144]{1,0:T(8,128)(2,1)S(1)}, u32[]{:S(2)}, u32[]{:S(2)}) collective-permute-start(bf16[16,6144]{1,0:T(8,128)(2,1)S(1)} %copy-done), channel_id=1, source_target_pairs={{0,16},{16,0},{32,48},{48,32},{64,80},{80,64},{96,112},{112,96},{1... | collective-permute-start | bytes 589832 | tf_op jit(solution)/shard_map/ppermute | solution.py:304
  29.5 0.7 %collective-permute-start.1 = (bf16[16,6144]{1,0:T(8,128)(2,1)S(1)}, bf16[16,6144]{1,0:T(8,128)(2,1)S(1)}, u32[]{:S(2)}, u32[]{:S(2)}) collective-permute-start(bf16[16,6144]{1,0:T(8,128)(2,1)S(1)} %copy-done), channel_id=1, source_target_pairs={{16,32},{32,16},{48,64},{64,48},{80,96},{96,80},{112,128},{128,112... | collective-permute-start | bytes 589832 | tf_op jit(solution)/shard_map/ppermute | solution.py:305
  30.2 0.0 copy-done.2
  30.2 0.2 sphere_rows.1.rows
  30.4 0.0 copy-start.1
  30.4 11.3 %all-to-all-done.1.sums = bf16[16,32,384]{2,1,0:T(8,128)(2,1)S(1)} async-done(((bf16[16,32,384]{2,1,0:T(8,128)(2,1)}), bf16[16,32,384]{2,1,0:T(8,128)(2,1)S(1)}, u32[]{:S(2)}, u32[]{:S(2)}) %all-to-all-start.1) | async-done | bytes 393248 | tf_op jit(solution)/shard_map/all_to_all | solution.py:317
  41.7 1.0 %couple.1 = bf16[16,16,384]{2,1,0:T(8,128)(2,1)} custom-call(bf16[256,512]{1,0:T(8,128)(2,1)S(1)} %sphere_rows.1.rows, bf16[16,32,384]{2,1,0:T(8,128)(2,1)S(1)} %all-to-all-done.1.sums), custom_call_target="tpu_custom_call" | custom-call | tf_op jit(solution)/shard_map/couple/pallas_call | solution.py:121
  42.7 0.0 copy-start.3
  42.7 6.7 %all-to-all-start.2 = ((bf16[16,16,384]{2,1,0:T(8,128)(2,1)}), bf16[16,16,384]{2,1,0:T(8,128)(2,1)S(1)}, u32[]{:S(2)}, u32[]{:S(2)}) async-start(bf16[16,16,384]{2,1,0:T(8,128)(2,1)} %couple.1), calls=%async_computation.2 | async-start | bytes 393216 | tf_op jit(solution)/shard_map/all_to_all | solution.py:321
  49.4 0.0 copy-start.4
  49.4 0.0 copy-start.5
  49.5 0.0 copy-start.6
  49.5 0.0 copy-start.8
  49.5 0.1 fusion.1.perm
  49.6 0.0 copy-done.1
  49.6 0.0 copy-done.3
  49.6 0.6 copy-done.4
  50.2 0.0 copy-done.5
  50.2 0.0 copy-done.6
  50.2 0.0 copy-done.8
  50.2 0.0 copy-start.7
  50.2 1.4 %prepare.1 = (bf16[4096,128]{1,0:T(8,128)(2,1)S(1)}, f32[512,128]{1,0:T(8,128)S(1)}, bf16[256,128]{1,0:T(8,128)(2,1)S(1)}, f32[16,24,128]{2,1,0:T(8,128)S(1)}, f32[16,24,128]{2,1,0:T(8,128)S(1)}) custom-call(s32[16]{0:T(128)S(1)} %copy-done.8, bf16[16,32,96]{2,1,0:T(8,128)(2,1)S(1)} %copy-done.3, bf16[32,96,96]{2,1,0:T(8,128)(2,1)S(1)} %copy-done.1, ...), custom_call_target="tpu_custom_call" | custom-call | tf_op jit(solution)/shard_map/prepare/pallas_call | solution.py:161
  51.6 0.0 collective-permute-done.side_a
  51.6 0.0 collective-permute-done.1.side_b
  51.6 0.0 copy-done.7
  51.6 8.5 %near.1 = f32[1024,128]{1,0:T(8,128)S(1)} custom-call(s32[16,32]{1,0:T(8,128)S(1)} %copy-done.7, s32[1]{0:T(128)} %bitcast.column, bf16[16,6144]{1,0:T(8,128)(2,1)S(1)} %collective-permute-done.side_a, bf16[16,6144]{1,0:T(8,128)(2,1)S(1)} %copy-done, bf16[16,6144]{1,0:T(8,128)(2,1)S(1)} %collective-permute-done.1.side_b, ...), custom_call_target="tpu_custom_call" | custom-call | tf_op jit(solution)/shard_map/near/pallas_call | solution.py:239
  60.1 0.0 all-to-all-done.2.got
  60.1 1.5 %tail.1 = bf16[16,6144]{1,0:T(8,128)(2,1)} custom-call(bf16[16,16,384]{2,1,0:T(8,128)(2,1)S(1)} %all-to-all-done.2.got, f32[1024,128]{1,0:T(8,128)S(1)} %near.1, bf16[16,6144]{1,0:T(8,128)(2,1)S(1)} %copy-done, f32[16,24,128]{2,1,0:T(8,128)S(1)} %get-tuple-element.16.tmat_re, f32[16,24,128]{2,1,0:T(8,128)S(1)} %get-tuple-element.17.tmat_im, ...), custom_call_target="tpu_custom_call" | custom-call | tf_op jit(solution)/shard_map/tail/pallas_call | solution.py:286
  (2 shorter events, 0.0 us)
Async XLA Ops:
  16.0 14.2 %copy-start.2 = (bf16[512,512]{1,0:T(8,128)(2,1)S(1)}, bf16[512,512]{1,0:T(8,128)(2,1)}, u32[]{:S(2)}) copy-start(bf16[512,512]{1,0:T(8,128)(2,1)} %coupling.1) | copy-start | bytes 1572868
  17.0 10.2 %copy-start = (bf16[16,6144]{1,0:T(8,128)(2,1)S(1)}, bf16[16,6144]{1,0:T(8,128)(2,1)}, u32[]{:S(2)}) copy-start(bf16[16,6144]{1,0:T(8,128)(2,1)} %x.3) | copy-start | bytes 589828
  17.0 24.7 %all-to-all-start.1 = ((bf16[16,32,384]{2,1,0:T(8,128)(2,1)}), bf16[16,32,384]{2,1,0:T(8,128)(2,1)S(1)}, u32[]{:S(2)}, u32[]{:S(2)}) async-start(bf16[16,32,384]{2,1,0:T(8,128)(2,1)} %get-tuple-element.13), calls=%async_computation.1 | async-start | bytes 786432 | tf_op jit(solution)/shard_map/all_to_all | solution.py:317
  27.2 24.5 %collective-permute-start = (bf16[16,6144]{1,0:T(8,128)(2,1)S(1)}, bf16[16,6144]{1,0:T(8,128)(2,1)S(1)}, u32[]{:S(2)}, u32[]{:S(2)}) collective-permute-start(bf16[16,6144]{1,0:T(8,128)(2,1)S(1)} %copy-done), channel_id=1, source_target_pairs={{0,16},{16,0},{32,48},{48,32},{64,80},{80,64},{96,112},{112,96},{1... | collective-permute-start | bytes 589832 | tf_op jit(solution)/shard_map/ppermute | solution.py:304
  29.5 22.1 %collective-permute-start.1 = (bf16[16,6144]{1,0:T(8,128)(2,1)S(1)}, bf16[16,6144]{1,0:T(8,128)(2,1)S(1)}, u32[]{:S(2)}, u32[]{:S(2)}) collective-permute-start(bf16[16,6144]{1,0:T(8,128)(2,1)S(1)} %copy-done), channel_id=1, source_target_pairs={{16,32},{32,16},{48,64},{64,48},{80,96},{96,80},{112,128},{128,112... | collective-permute-start | bytes 589832 | tf_op jit(solution)/shard_map/ppermute | solution.py:305
  30.4 19.2 %copy-start.1 = (bf16[32,96,96]{2,1,0:T(8,128)(2,1)S(1)}, bf16[32,96,96]{2,1,0:T(8,128)(2,1)}, u32[]{:S(2)}) copy-start(bf16[32,96,96]{2,1,0:T(8,128)(2,1)} %rot.1) | copy-start | bytes 1769476
  42.7 6.9 %copy-start.3 = (bf16[16,32,96]{2,1,0:T(8,128)(2,1)S(1)}, bf16[16,32,96]{2,1,0:T(8,128)(2,1)}, u32[]{:S(2)}) copy-start(bf16[16,32,96]{2,1,0:T(8,128)(2,1)} %axial.1) | copy-start | bytes 294916
  42.7 17.4 %all-to-all-start.2 = ((bf16[16,16,384]{2,1,0:T(8,128)(2,1)}), bf16[16,16,384]{2,1,0:T(8,128)(2,1)S(1)}, u32[]{:S(2)}, u32[]{:S(2)}) async-start(bf16[16,16,384]{2,1,0:T(8,128)(2,1)} %couple.1), calls=%async_computation.2 | async-start | bytes 393216 | tf_op jit(solution)/shard_map/all_to_all | solution.py:321
  49.4 0.7 %copy-start.4 = (bf16[96,96]{1,0:T(8,128)(2,1)S(1)}, bf16[96,96]{1,0:T(8,128)(2,1)}, u32[]{:S(2)}) copy-start(bf16[96,96]{1,0:T(8,128)(2,1)} %out_map.1) | copy-start | bytes 55300
  49.4 0.7 %copy-start.5 = (bf16[96,96]{1,0:T(8,128)(2,1)S(1)}, bf16[96,96]{1,0:T(8,128)(2,1)}, u32[]{:S(2)}) copy-start(bf16[96,96]{1,0:T(8,128)(2,1)} %in_map.1) | copy-start | bytes 55300
  49.5 0.7 %copy-start.6 = (f32[16,96]{1,0:T(8,128)S(1)}, f32[16,96]{1,0:T(8,128)}, u32[]{:S(2)}) copy-start(f32[16,96]{1,0:T(8,128)} %tmat.1) | copy-start | bytes 18436
  49.5 0.7 %copy-start.8 = (s32[16]{0:T(128)S(1)}, s32[16]{0:T(128)}, u32[]{:S(2)}) copy-start(s32[16]{0:T(128)} %counts.1) | copy-start | bytes 196
  50.2 1.5 %copy-start.7 = (s32[16,32]{1,0:T(8,128)S(1)}, s32[16,32]{1,0:T(8,128)}, u32[]{:S(2)}) copy-start(s32[16,32]{1,0:T(8,128)} %nbr.1) | copy-start | bytes 6148

commit v6 on v5

--- a/solution.py
+++ b/solution.py
@@ -13,6 +13,7 @@
 NBG = 2
 LANES = 128
 HALF = 64
+PITCH = 72
 UNROLL = 8
 
 
@@ -27,7 +28,7 @@
 def to_planes(rows, planes, base):
     sd, width = rows.shape
     for t in range(width // LANES):
-        planes[pl.ds(base * HALF + t, sd, stride=HALF), :] = rows[:, t * LANES:(t + 1) * LANES].astype(F32)
+        planes[pl.ds(base * PITCH + t, sd, stride=PITCH), :] = rows[:, t * LANES:(t + 1) * LANES].astype(F32)
 
 
 def swap_halves(a):
@@ -188,7 +189,9 @@
             copies[c // 2].wait()
         to_planes(own if c == 1 else sides[c // 2], planes, 0)
         for s in range(0, sd, 2):
-            both = planes[s * HALF:(s + 2) * HALF, :].T
+            both = jnp.concatenate(
+                [planes[r * PITCH:r * PITCH + HALF, :] for r in (s, s + 1)], axis=0
+            ).T
             top, bottom = both[:HALF], both[HALF:]
             cand[base + s] = jnp.where(lane, top, swap_halves(bottom)).astype(BF16)
             cand[base + s + 1] = jnp.where(lane, swap_halves(top), bottom).astype(BF16)
@@ -243,7 +246,7 @@
         out_specs=vmem,
         scratch_shapes=[
             pltpu.VMEM((2, *own.shape), BF16),
-            pltpu.VMEM((sd * HALF, LANES), F32),
+            pltpu.VMEM((sd * PITCH, LANES), F32),
             pltpu.VMEM((3 * sd, HALF, LANES), BF16),
             pltpu.VMEM((UNROLL, 2 * LANES, 2 * LANES), BF16),
             pltpu.VMEM((sd * HALF, LANES), F32),
@@ -264,21 +267,21 @@
         part = got[g]
         for q in range(per):
             t = g * per + q
-            planes[pl.ds(t, sd, stride=HALF), :] = part[:, q * LANES:(q + 1) * LANES].astype(F32)
+            planes[pl.ds(t, sd, stride=PITCH), :] = part[:, q * LANES:(q + 1) * LANES].astype(F32)
     hi = maps[:LANES]
     lo = maps[LANES:]
     for s in range(sd):
-        loc = planes[s * HALF:(s + 1) * HALF, :]
+        loc = planes[s * PITCH:s * PITCH + HALF, :]
         both = jnp.concatenate([loc, swap_halves(loc)], axis=0).astype(BF16)
         prod = dot(hi, both) + dot(lo, both)
         field = near[s * HALF:(s + 1) * HALF, :] + jnp.where(lane, prod[:HALF], prod[HALF:])
         ur, ui = field[:half], field[half:2 * half]
         tr, ti = tmat_re[s], tmat_im[s]
-        planes[s * HALF:s * HALF + half, :] = tr * ur - ti * ui
-        planes[s * HALF + half:s * HALF + 2 * half, :] = tr * ui + ti * ur
+        planes[s * PITCH:s * PITCH + half, :] = tr * ur - ti * ui
+        planes[s * PITCH + half:s * PITCH + 2 * half, :] = tr * ui + ti * ur
     for t in range(2 * half):
         cols = slice(t * LANES, (t + 1) * LANES)
-        out[:, cols] = (x[:, cols].astype(F32) - planes[pl.ds(t, sd, stride=HALF), :]).astype(BF16)
+        out[:, cols] = (x[:, cols].astype(F32) - planes[pl.ds(t, sd, stride=PITCH), :]).astype(BF16)
 
 
 def tail(got, near, coeffs, tmat_re, tmat_im, maps):
@@ -286,7 +289,7 @@
     return pl.pallas_call(
         tail_kernel,
         out_shape=jax.ShapeDtypeStruct(coeffs.shape, BF16),
-        scratch_shapes=[pltpu.VMEM((sd * HALF, LANES), F32)],
+        scratch_shapes=[pltpu.VMEM((sd * PITCH, LANES), F32)],
         compiler_params=params(),
         name="tail",
     )(got, near, coeffs, tmat_re, tmat_im, maps)

time: 62.1 us -> 61.4 us (0.989)
  Pallas kernels: 15.2 us -> 14.5 us
  transfers between devices with their start and end apart: 4 -> 4, of which waited for: 1 -> 1; matrix products, arithmetic and copies ran while one was open for 0% -> 0% of each run, Pallas kernels for 18% -> 17%
where the time goes in v6:
time: 61.4 us; the launch traced here: 61 us
  starting transfers between devices  19.9 us (32%)
  Pallas kernels  14.5 us (24%)
  blocking collectives  14.3 us (23%)
  waiting for transfers between devices  11.3 us (18%)
  local copies, waits for them, and re-layouts  0.62 us (1%)
    all_to_all x1, blocking collectives, shards(): got = lax.all_to_all(sent, 'grp', 0, 0, tiled=True)  14.3 us
    all_to_all x1, waiting for transfers between devices, shards(): every = lax.all_to_all(sums, 'cells', 0, 0, tiled=True)  11.3 us
    all_to_all x1, starting transfers between devices, shards(): every = lax.all_to_all(sums, 'cells', 0, 0, tiled=True)  10.2 us
    pallas_call x1, Pallas kernels, near_field(): pl.pallas_call(near_kernel, out_shape=jax.ShapeDtypeStruct((sd * HALF, LA...  8.01 us
    all_to_all x1, starting transfers between devices, shards(): mine = lax.all_to_all(local, 'grp', 0, 0, tiled=True)  6.72 us
    ppermute x1, starting transfers between devices, shards(): near_a = lax.ppermute(coeffs, 'cells', first)  2.35 us
    pallas_call x1, Pallas kernels, pack(): pl.pallas_call(pack_kernel, out_shape=jax.ShapeDtypeStruct((ngrp, sd, wid...  1.66 us
    pallas_call x1, Pallas kernels, prepare(): pl.pallas_call(prep_kernel, out_shape=(jax.ShapeDtypeStruct((slots * LANE...  1.43 us
  transfers between devices with their start and end apart: 4, of which 1 were waited for; matrix products, arithmetic and copies ran while one was open for 0% of the time, Pallas kernels for 17%

profile of v6, /device:TPU:1, one launch (start us, length us, event | category | flops | bytes accessed | tf_op | source)
XLA Modules:
  0.0 61.0 jit_solution(3868292535675782544)
XLA Ops:
  0.0 1.7 %pack.1 = bf16[16,16,512]{2,1,0:T(8,128)(2,1)} custom-call(s32[16]{0:T(128)} %boxes.1, bf16[16,6144]{1,0:T(8,128)(2,1)} %x.3), custom_call_target="tpu_custom_call" | custom-call | tf_op jit(solution)/shard_map/pack/pallas_call | solution.py:54
  1.7 14.3 %all_to_all.15.got = bf16[16,16,512]{2,1,0:T(8,128)(2,1)S(1)} all-to-all(bf16[16,16,512]{2,1,0:T(8,128)(2,1)} %pack.1), channel_id=1, replica_groups=mesh['cells'=16,'grp'=16] {'grp'}, dimensions={0} | all-to-all | bytes 524288 | tf_op jit(solution)/shard_map/all_to_all | solution.py:310
  16.0 0.0 copy-start.2
  16.0 1.0 %box_sums.1 = (bf16[16,32,384]{2,1,0:T(8,128)(2,1)}, bf16[256,32]{1,0:T(8,128)(2,1)S(1)}) custom-call(bf16[16,16,512]{2,1,0:T(8,128)(2,1)S(1)} %all_to_all.15.got), custom_call_target="tpu_custom_call" | custom-call | tf_op jit(solution)/shard_map/box_sums/pallas_call | solution.py:79
  17.0 0.0 copy-start
  17.0 10.2 %all-to-all-start.1 = ((bf16[16,32,384]{2,1,0:T(8,128)(2,1)}), bf16[16,32,384]{2,1,0:T(8,128)(2,1)S(1)}, u32[]{:S(2)}, u32[]{:S(2)}) async-start(bf16[16,32,384]{2,1,0:T(8,128)(2,1)} %get-tuple-element.13), calls=%async_computation.1 | async-start | bytes 786432 | tf_op jit(solution)/shard_map/all_to_all | solution.py:320
  27.1 0.0 copy-done
  27.2 2.3 %collective-permute-start = (bf16[16,6144]{1,0:T(8,128)(2,1)S(1)}, bf16[16,6144]{1,0:T(8,128)(2,1)S(1)}, u32[]{:S(2)}, u32[]{:S(2)}) collective-permute-start(bf16[16,6144]{1,0:T(8,128)(2,1)S(1)} %copy-done), channel_id=1, source_target_pairs={{0,16},{16,0},{32,48},{48,32},{64,80},{80,64},{96,112},{112,96},{1... | collective-permute-start | bytes 589832 | tf_op jit(solution)/shard_map/ppermute | solution.py:307
  29.5 0.7 %collective-permute-start.1 = (bf16[16,6144]{1,0:T(8,128)(2,1)S(1)}, bf16[16,6144]{1,0:T(8,128)(2,1)S(1)}, u32[]{:S(2)}, u32[]{:S(2)}) collective-permute-start(bf16[16,6144]{1,0:T(8,128)(2,1)S(1)} %copy-done), channel_id=1, source_target_pairs={{16,32},{32,16},{48,64},{64,48},{80,96},{96,80},{112,128},{128,112... | collective-permute-start | bytes 589832 | tf_op jit(solution)/shard_map/ppermute | solution.py:308
  30.2 0.0 copy-done.2
  30.2 0.2 sphere_rows.1.rows
  30.4 0.0 copy-start.1
  30.4 11.3 %all-to-all-done.1.sums = bf16[16,32,384]{2,1,0:T(8,128)(2,1)S(1)} async-done(((bf16[16,32,384]{2,1,0:T(8,128)(2,1)}), bf16[16,32,384]{2,1,0:T(8,128)(2,1)S(1)}, u32[]{:S(2)}, u32[]{:S(2)}) %all-to-all-start.1) | async-done | bytes 393248 | tf_op jit(solution)/shard_map/all_to_all | solution.py:320
  41.7 1.0 %couple.1 = bf16[16,16,384]{2,1,0:T(8,128)(2,1)} custom-call(bf16[256,512]{1,0:T(8,128)(2,1)S(1)} %sphere_rows.1.rows, bf16[16,32,384]{2,1,0:T(8,128)(2,1)S(1)} %all-to-all-done.1.sums), custom_call_target="tpu_custom_call" | custom-call | tf_op jit(solution)/shard_map/couple/pallas_call | solution.py:122
  42.7 0.0 copy-start.3
  42.7 6.7 %all-to-all-start.2 = ((bf16[16,16,384]{2,1,0:T(8,128)(2,1)}), bf16[16,16,384]{2,1,0:T(8,128)(2,1)S(1)}, u32[]{:S(2)}, u32[]{:S(2)}) async-start(bf16[16,16,384]{2,1,0:T(8,128)(2,1)} %couple.1), calls=%async_computation.2 | async-start | bytes 393216 | tf_op jit(solution)/shard_map/all_to_all | solution.py:324
  49.4 0.0 copy-start.4
  49.4 0.0 copy-start.5
  49.5 0.0 copy-start.6
  49.5 0.0 copy-start.8
  49.5 0.1 fusion.1.perm
  49.6 0.0 copy-done.1
  49.6 0.0 copy-done.3
  49.6 0.6 copy-done.4
  50.2 0.0 copy-done.5
  50.2 0.0 copy-done.6
  50.2 0.0 copy-done.8
  50.2 0.0 copy-start.7
  50.2 1.4 %prepare.1 = (bf16[4096,128]{1,0:T(8,128)(2,1)S(1)}, f32[512,128]{1,0:T(8,128)S(1)}, bf16[256,128]{1,0:T(8,128)(2,1)S(1)}, f32[16,24,128]{2,1,0:T(8,128)S(1)}, f32[16,24,128]{2,1,0:T(8,128)S(1)}) custom-call(s32[16]{0:T(128)S(1)} %copy-done.8, bf16[16,32,96]{2,1,0:T(8,128)(2,1)S(1)} %copy-done.3, bf16[32,96,96]{2,1,0:T(8,128)(2,1)S(1)} %copy-done.1, ...), custom_call_target="tpu_custom_call" | custom-call | tf_op jit(solution)/shard_map/prepare/pallas_call | solution.py:162
  51.6 0.0 collective-permute-done.side_a
  51.6 0.0 collective-permute-done.1.side_b
  51.6 0.0 copy-done.7
  51.6 8.0 %near.1 = f32[1024,128]{1,0:T(8,128)S(1)} custom-call(s32[16,32]{1,0:T(8,128)S(1)} %copy-done.7, s32[1]{0:T(128)} %bitcast.column, bf16[16,6144]{1,0:T(8,128)(2,1)S(1)} %collective-permute-done.side_a, bf16[16,6144]{1,0:T(8,128)(2,1)S(1)} %copy-done, bf16[16,6144]{1,0:T(8,128)(2,1)S(1)} %collective-permute-done.1.side_b, ...), custom_call_target="tpu_custom_call" | custom-call | tf_op jit(solution)/shard_map/near/pallas_call | solution.py:242
  59.7 0.0 all-to-all-done.2.got
  59.7 1.3 %tail.1 = bf16[16,6144]{1,0:T(8,128)(2,1)} custom-call(bf16[16,16,384]{2,1,0:T(8,128)(2,1)S(1)} %all-to-all-done.2.got, f32[1024,128]{1,0:T(8,128)S(1)} %near.1, bf16[16,6144]{1,0:T(8,128)(2,1)S(1)} %copy-done, f32[16,24,128]{2,1,0:T(8,128)S(1)} %get-tuple-element.16.tmat_re, f32[16,24,128]{2,1,0:T(8,128)S(1)} %get-tuple-element.17.tmat_im, ...), custom_call_target="tpu_custom_call" | custom-call | tf_op jit(solution)/shard_map/tail/pallas_call | solution.py:289
  (2 shorter events, 0.0 us)
Async XLA Ops:
  16.0 14.2 %copy-start.2 = (bf16[512,512]{1,0:T(8,128)(2,1)S(1)}, bf16[512,512]{1,0:T(8,128)(2,1)}, u32[]{:S(2)}) copy-start(bf16[512,512]{1,0:T(8,128)(2,1)} %coupling.1) | copy-start | bytes 1572868
  17.0 10.2 %copy-start = (bf16[16,6144]{1,0:T(8,128)(2,1)S(1)}, bf16[16,6144]{1,0:T(8,128)(2,1)}, u32[]{:S(2)}) copy-start(bf16[16,6144]{1,0:T(8,128)(2,1)} %x.3) | copy-start | bytes 589828
  17.0 24.7 %all-to-all-start.1 = ((bf16[16,32,384]{2,1,0:T(8,128)(2,1)}), bf16[16,32,384]{2,1,0:T(8,128)(2,1)S(1)}, u32[]{:S(2)}, u32[]{:S(2)}) async-start(bf16[16,32,384]{2,1,0:T(8,128)(2,1)} %get-tuple-element.13), calls=%async_computation.1 | async-start | bytes 786432 | tf_op jit(solution)/shard_map/all_to_all | solution.py:320
  27.2 24.5 %collective-permute-start = (bf16[16,6144]{1,0:T(8,128)(2,1)S(1)}, bf16[16,6144]{1,0:T(8,128)(2,1)S(1)}, u32[]{:S(2)}, u32[]{:S(2)}) collective-permute-start(bf16[16,6144]{1,0:T(8,128)(2,1)S(1)} %copy-done), channel_id=1, source_target_pairs={{0,16},{16,0},{32,48},{48,32},{64,80},{80,64},{96,112},{112,96},{1... | collective-permute-start | bytes 589832 | tf_op jit(solution)/shard_map/ppermute | solution.py:307
  29.5 22.1 %collective-permute-start.1 = (bf16[16,6144]{1,0:T(8,128)(2,1)S(1)}, bf16[16,6144]{1,0:T(8,128)(2,1)S(1)}, u32[]{:S(2)}, u32[]{:S(2)}) collective-permute-start(bf16[16,6144]{1,0:T(8,128)(2,1)S(1)} %copy-done), channel_id=1, source_target_pairs={{16,32},{32,16},{48,64},{64,48},{80,96},{96,80},{112,128},{128,112... | collective-permute-start | bytes 589832 | tf_op jit(solution)/shard_map/ppermute | solution.py:308
  30.4 19.2 %copy-start.1 = (bf16[32,96,96]{2,1,0:T(8,128)(2,1)S(1)}, bf16[32,96,96]{2,1,0:T(8,128)(2,1)}, u32[]{:S(2)}) copy-start(bf16[32,96,96]{2,1,0:T(8,128)(2,1)} %rot.1) | copy-start | bytes 1769476
  42.7 6.9 %copy-start.3 = (bf16[16,32,96]{2,1,0:T(8,128)(2,1)S(1)}, bf16[16,32,96]{2,1,0:T(8,128)(2,1)}, u32[]{:S(2)}) copy-start(bf16[16,32,96]{2,1,0:T(8,128)(2,1)} %axial.1) | copy-start | bytes 294916
  42.7 17.0 %all-to-all-start.2 = ((bf16[16,16,384]{2,1,0:T(8,128)(2,1)}), bf16[16,16,384]{2,1,0:T(8,128)(2,1)S(1)}, u32[]{:S(2)}, u32[]{:S(2)}) async-start(bf16[16,16,384]{2,1,0:T(8,128)(2,1)} %couple.1), calls=%async_computation.2 | async-start | bytes 393216 | tf_op jit(solution)/shard_map/all_to_all | solution.py:324
  49.4 0.7 %copy-start.4 = (bf16[96,96]{1,0:T(8,128)(2,1)S(1)}, bf16[96,96]{1,0:T(8,128)(2,1)}, u32[]{:S(2)}) copy-start(bf16[96,96]{1,0:T(8,128)(2,1)} %out_map.1) | copy-start | bytes 55300
  49.4 0.7 %copy-start.5 = (bf16[96,96]{1,0:T(8,128)(2,1)S(1)}, bf16[96,96]{1,0:T(8,128)(2,1)}, u32[]{:S(2)}) copy-start(bf16[96,96]{1,0:T(8,128)(2,1)} %in_map.1) | copy-start | bytes 55300
  49.5 0.7 %copy-start.6 = (f32[16,96]{1,0:T(8,128)S(1)}, f32[16,96]{1,0:T(8,128)}, u32[]{:S(2)}) copy-start(f32[16,96]{1,0:T(8,128)} %tmat.1) | copy-start | bytes 18436
  49.5 0.7 %copy-start.8 = (s32[16]{0:T(128)S(1)}, s32[16]{0:T(128)}, u32[]{:S(2)}) copy-start(s32[16]{0:T(128)} %counts.1) | copy-start | bytes 196
  50.2 1.5 %copy-start.7 = (s32[16,32]{1,0:T(8,128)S(1)}, s32[16,32]{1,0:T(8,128)}, u32[]{:S(2)}) copy-start(s32[16,32]{1,0:T(8,128)} %nbr.1) | copy-start | bytes 6148

commit v7 on v6

--- a/solution.py
+++ b/solution.py
@@ -15,6 +15,7 @@
 HALF = 64
 PITCH = 72
 UNROLL = 8
+PARTS = 4
 
 
 def dot(a, b, ca=1, cb=0):
@@ -257,7 +258,7 @@
     )(nbr, column, side_a, own, side_b, scale, turn)
 
 
-def tail_kernel(got, near, x, tmat_re, tmat_im, maps, out, planes):
+def tail_kernel(got, near, x, tmat_re, tmat_im, maps, out, planes, ready, sems):
     ngrp, sd, feat = got.shape
     per = feat // LANES
     lane = lax.broadcasted_iota(jnp.int32, (HALF, LANES), 1) < HALF
@@ -270,18 +271,34 @@
             planes[pl.ds(t, sd, stride=PITCH), :] = part[:, q * LANES:(q + 1) * LANES].astype(F32)
     hi = maps[:LANES]
     lo = maps[LANES:]
+    prods = []
+    for s in range(0, sd, 2):
+        pair = []
+        for r in (s, s + 1):
+            loc = planes[r * PITCH:r * PITCH + HALF, :]
+            pair.append(jnp.concatenate([loc, swap_halves(loc)], axis=0).astype(BF16))
+        both = jnp.concatenate(pair, axis=1)
+        prod = dot(hi, both) + dot(lo, both)
+        prods += [prod[:, :LANES], prod[:, LANES:]]
     for s in range(sd):
-        loc = planes[s * PITCH:s * PITCH + HALF, :]
-        both = jnp.concatenate([loc, swap_halves(loc)], axis=0).astype(BF16)
-        prod = dot(hi, both) + dot(lo, both)
+        prod = prods[s]
         field = near[s * HALF:(s + 1) * HALF, :] + jnp.where(lane, prod[:HALF], prod[HALF:])
         ur, ui = field[:half], field[half:2 * half]
         tr, ti = tmat_re[s], tmat_im[s]
         planes[s * PITCH:s * PITCH + half, :] = tr * ur - ti * ui
         planes[s * PITCH + half:s * PITCH + 2 * half, :] = tr * ui + ti * ur
+    chunk = 2 * half // PARTS
+    copies = []
     for t in range(2 * half):
         cols = slice(t * LANES, (t + 1) * LANES)
-        out[:, cols] = (x[:, cols].astype(F32) - planes[pl.ds(t, sd, stride=PITCH), :]).astype(BF16)
+        ready[:, cols] = (x[:, cols].astype(F32) - planes[pl.ds(t, sd, stride=PITCH), :]).astype(BF16)
+        if (t + 1) % chunk == 0:
+            n = t // chunk
+            span = pl.ds(n * chunk * LANES, chunk * LANES)
+            copies.append(pltpu.make_async_copy(ready.at[:, span], out.at[:, span], sems.at[n]))
+            copies[-1].start()
+    for copy in copies:
+        copy.wait()
 
 
 def tail(got, near, coeffs, tmat_re, tmat_im, maps):
@@ -289,7 +306,12 @@
     return pl.pallas_call(
         tail_kernel,
         out_shape=jax.ShapeDtypeStruct(coeffs.shape, BF16),
-        scratch_shapes=[pltpu.VMEM((sd * PITCH, LANES), F32)],
+        out_specs=pl.BlockSpec(memory_space=pltpu.HBM),
+        scratch_shapes=[
+            pltpu.VMEM((sd * PITCH, LANES), F32),
+            pltpu.VMEM(coeffs.shape, BF16),
+            pltpu.SemaphoreType.DMA((PARTS,)),
+        ],
         compiler_params=params(),
         name="tail",
     )(got, near, coeffs, tmat_re, tmat_im, maps)

time: 61.4 us -> 61.4 us (level)
  no operation moved by 1% of the time
where the time goes in v7:
time: 61.4 us; the launch traced here: 61 us
  starting transfers between devices  19.9 us (32%)
  Pallas kernels  14.5 us (24%)
  blocking collectives  14.3 us (23%)
  waiting for transfers between devices  11.3 us (18%)
  local copies, waits for them, and re-layouts  0.62 us (1%)
    all_to_all x1, blocking collectives, shards(): got = lax.all_to_all(sent, 'grp', 0, 0, tiled=True)  14.3 us
    all_to_all x1, waiting for transfers between devices, shards(): every = lax.all_to_all(sums, 'cells', 0, 0, tiled=True)  11.3 us
    all_to_all x1, starting transfers between devices, shards(): every = lax.all_to_all(sums, 'cells', 0, 0, tiled=True)  10.2 us
    pallas_call x1, Pallas kernels, near_field(): pl.pallas_call(near_kernel, out_shape=jax.ShapeDtypeStruct((sd * HALF, LA...  8.01 us
    all_to_all x1, starting transfers between devices, shards(): mine = lax.all_to_all(local, 'grp', 0, 0, tiled=True)  6.72 us
    ppermute x1, starting transfers between devices, shards(): near_a = lax.ppermute(coeffs, 'cells', first)  2.35 us
    pallas_call x1, Pallas kernels, pack(): pl.pallas_call(pack_kernel, out_shape=jax.ShapeDtypeStruct((ngrp, sd, wid...  1.66 us
    pallas_call x1, Pallas kernels, prepare(): pl.pallas_call(prep_kernel, out_shape=(jax.ShapeDtypeStruct((slots * LANE...  1.43 us
  transfers between devices with their start and end apart: 4, of which 1 were waited for; matrix products, arithmetic and copies ran while one was open for 0% of the time, Pallas kernels for 17%

profile of v7, /device:TPU:1, one launch (start us, length us, event | category | flops | bytes accessed | tf_op | source)
XLA Modules:
  0.0 61.0 jit_solution(9156908041917208825)
XLA Ops:
  0.0 1.7 %pack.1 = bf16[16,16,512]{2,1,0:T(8,128)(2,1)} custom-call(s32[16]{0:T(128)} %boxes.1, bf16[16,6144]{1,0:T(8,128)(2,1)} %x.3), custom_call_target="tpu_custom_call" | custom-call | tf_op jit(solution)/shard_map/pack/pallas_call | solution.py:55
  1.7 14.3 %all_to_all.15.got = bf16[16,16,512]{2,1,0:T(8,128)(2,1)S(1)} all-to-all(bf16[16,16,512]{2,1,0:T(8,128)(2,1)} %pack.1), channel_id=1, replica_groups=mesh['cells'=16,'grp'=16] {'grp'}, dimensions={0} | all-to-all | bytes 524288 | tf_op jit(solution)/shard_map/all_to_all | solution.py:332
  16.0 0.0 copy-start.2
  16.0 1.0 %box_sums.1 = (bf16[16,32,384]{2,1,0:T(8,128)(2,1)}, bf16[256,32]{1,0:T(8,128)(2,1)S(1)}) custom-call(bf16[16,16,512]{2,1,0:T(8,128)(2,1)S(1)} %all_to_all.15.got), custom_call_target="tpu_custom_call" | custom-call | tf_op jit(solution)/shard_map/box_sums/pallas_call | solution.py:80
  17.0 0.0 copy-start
  17.0 10.2 %all-to-all-start.1 = ((bf16[16,32,384]{2,1,0:T(8,128)(2,1)}), bf16[16,32,384]{2,1,0:T(8,128)(2,1)S(1)}, u32[]{:S(2)}, u32[]{:S(2)}) async-start(bf16[16,32,384]{2,1,0:T(8,128)(2,1)} %get-tuple-element.13), calls=%async_computation.1 | async-start | bytes 786432 | tf_op jit(solution)/shard_map/all_to_all | solution.py:342
  27.1 0.0 copy-done
  27.2 2.3 %collective-permute-start = (bf16[16,6144]{1,0:T(8,128)(2,1)S(1)}, bf16[16,6144]{1,0:T(8,128)(2,1)S(1)}, u32[]{:S(2)}, u32[]{:S(2)}) collective-permute-start(bf16[16,6144]{1,0:T(8,128)(2,1)S(1)} %copy-done), channel_id=1, source_target_pairs={{0,16},{16,0},{32,48},{48,32},{64,80},{80,64},{96,112},{112,96},{1... | collective-permute-start | bytes 589832 | tf_op jit(solution)/shard_map/ppermute | solution.py:329
  29.5 0.7 %collective-permute-start.1 = (bf16[16,6144]{1,0:T(8,128)(2,1)S(1)}, bf16[16,6144]{1,0:T(8,128)(2,1)S(1)}, u32[]{:S(2)}, u32[]{:S(2)}) collective-permute-start(bf16[16,6144]{1,0:T(8,128)(2,1)S(1)} %copy-done), channel_id=1, source_target_pairs={{16,32},{32,16},{48,64},{64,48},{80,96},{96,80},{112,128},{128,112... | collective-permute-start | bytes 589832 | tf_op jit(solution)/shard_map/ppermute | solution.py:330
  30.2 0.0 copy-done.2
  30.2 0.2 sphere_rows.1.rows
  30.4 0.0 copy-start.1
  30.4 11.3 %all-to-all-done.1.sums = bf16[16,32,384]{2,1,0:T(8,128)(2,1)S(1)} async-done(((bf16[16,32,384]{2,1,0:T(8,128)(2,1)}), bf16[16,32,384]{2,1,0:T(8,128)(2,1)S(1)}, u32[]{:S(2)}, u32[]{:S(2)}) %all-to-all-start.1) | async-done | bytes 393248 | tf_op jit(solution)/shard_map/all_to_all | solution.py:342
  41.7 1.0 %couple.1 = bf16[16,16,384]{2,1,0:T(8,128)(2,1)} custom-call(bf16[256,512]{1,0:T(8,128)(2,1)S(1)} %sphere_rows.1.rows, bf16[16,32,384]{2,1,0:T(8,128)(2,1)S(1)} %all-to-all-done.1.sums), custom_call_target="tpu_custom_call" | custom-call | tf_op jit(solution)/shard_map/couple/pallas_call | solution.py:123
  42.7 0.0 copy-start.3
  42.7 6.7 %all-to-all-start.2 = ((bf16[16,16,384]{2,1,0:T(8,128)(2,1)}), bf16[16,16,384]{2,1,0:T(8,128)(2,1)S(1)}, u32[]{:S(2)}, u32[]{:S(2)}) async-start(bf16[16,16,384]{2,1,0:T(8,128)(2,1)} %couple.1), calls=%async_computation.2 | async-start | bytes 393216 | tf_op jit(solution)/shard_map/all_to_all | solution.py:346
  49.4 0.0 copy-start.4
  49.4 0.0 copy-start.5
  49.5 0.0 copy-start.6
  49.5 0.0 copy-start.8
  49.5 0.1 fusion.1.perm
  49.6 0.0 copy-done.1
  49.6 0.0 copy-done.3
  49.6 0.6 copy-done.4
  50.2 0.0 copy-done.5
  50.2 0.0 copy-done.6
  50.2 0.0 copy-done.8
  50.2 0.0 copy-start.7
  50.2 1.4 %prepare.1 = (bf16[4096,128]{1,0:T(8,128)(2,1)S(1)}, f32[512,128]{1,0:T(8,128)S(1)}, bf16[256,128]{1,0:T(8,128)(2,1)S(1)}, f32[16,24,128]{2,1,0:T(8,128)S(1)}, f32[16,24,128]{2,1,0:T(8,128)S(1)}) custom-call(s32[16]{0:T(128)S(1)} %copy-done.8, bf16[16,32,96]{2,1,0:T(8,128)(2,1)S(1)} %copy-done.3, bf16[32,96,96]{2,1,0:T(8,128)(2,1)S(1)} %copy-done.1, ...), custom_call_target="tpu_custom_call" | custom-call | tf_op jit(solution)/shard_map/prepare/pallas_call | solution.py:163
  51.6 0.0 collective-permute-done.side_a
  51.6 0.0 collective-permute-done.1.side_b
  51.6 0.0 copy-done.7
  51.6 8.0 %near.1 = f32[1024,128]{1,0:T(8,128)S(1)} custom-call(s32[16,32]{1,0:T(8,128)S(1)} %copy-done.7, s32[1]{0:T(128)} %bitcast.column, bf16[16,6144]{1,0:T(8,128)(2,1)S(1)} %collective-permute-done.side_a, bf16[16,6144]{1,0:T(8,128)(2,1)S(1)} %copy-done, bf16[16,6144]{1,0:T(8,128)(2,1)S(1)} %collective-permute-done.1.side_b, ...), custom_call_target="tpu_custom_call" | custom-call | tf_op jit(solution)/shard_map/near/pallas_call | solution.py:243
  59.7 0.0 all-to-all-done.2.got
  59.7 1.3 %tail.1 = bf16[16,6144]{1,0:T(8,128)(2,1)} custom-call(bf16[16,16,384]{2,1,0:T(8,128)(2,1)S(1)} %all-to-all-done.2.got, f32[1024,128]{1,0:T(8,128)S(1)} %near.1, bf16[16,6144]{1,0:T(8,128)(2,1)S(1)} %copy-done, f32[16,24,128]{2,1,0:T(8,128)S(1)} %get-tuple-element.16.tmat_re, f32[16,24,128]{2,1,0:T(8,128)S(1)} %get-tuple-element.17.tmat_im, ...), custom_call_target="tpu_custom_call" | custom-call | tf_op jit(solution)/shard_map/tail/pallas_call | solution.py:306
  (2 shorter events, 0.0 us)
Async XLA Ops:
  16.0 14.2 %copy-start.2 = (bf16[512,512]{1,0:T(8,128)(2,1)S(1)}, bf16[512,512]{1,0:T(8,128)(2,1)}, u32[]{:S(2)}) copy-start(bf16[512,512]{1,0:T(8,128)(2,1)} %coupling.1) | copy-start | bytes 1572868
  17.0 10.2 %copy-start = (bf16[16,6144]{1,0:T(8,128)(2,1)S(1)}, bf16[16,6144]{1,0:T(8,128)(2,1)}, u32[]{:S(2)}) copy-start(bf16[16,6144]{1,0:T(8,128)(2,1)} %x.3) | copy-start | bytes 589828
  17.0 24.7 %all-to-all-start.1 = ((bf16[16,32,384]{2,1,0:T(8,128)(2,1)}), bf16[16,32,384]{2,1,0:T(8,128)(2,1)S(1)}, u32[]{:S(2)}, u32[]{:S(2)}) async-start(bf16[16,32,384]{2,1,0:T(8,128)(2,1)} %get-tuple-element.13), calls=%async_computation.1 | async-start | bytes 786432 | tf_op jit(solution)/shard_map/all_to_all | solution.py:342
  27.2 24.5 %collective-permute-start = (bf16[16,6144]{1,0:T(8,128)(2,1)S(1)}, bf16[16,6144]{1,0:T(8,128)(2,1)S(1)}, u32[]{:S(2)}, u32[]{:S(2)}) collective-permute-start(bf16[16,6144]{1,0:T(8,128)(2,1)S(1)} %copy-done), channel_id=1, source_target_pairs={{0,16},{16,0},{32,48},{48,32},{64,80},{80,64},{96,112},{112,96},{1... | collective-permute-start | bytes 589832 | tf_op jit(solution)/shard_map/ppermute | solution.py:329
  29.5 22.1 %collective-permute-start.1 = (bf16[16,6144]{1,0:T(8,128)(2,1)S(1)}, bf16[16,6144]{1,0:T(8,128)(2,1)S(1)}, u32[]{:S(2)}, u32[]{:S(2)}) collective-permute-start(bf16[16,6144]{1,0:T(8,128)(2,1)S(1)} %copy-done), channel_id=1, source_target_pairs={{16,32},{32,16},{48,64},{64,48},{80,96},{96,80},{112,128},{128,112... | collective-permute-start | bytes 589832 | tf_op jit(solution)/shard_map/ppermute | solution.py:330
  30.4 19.2 %copy-start.1 = (bf16[32,96,96]{2,1,0:T(8,128)(2,1)S(1)}, bf16[32,96,96]{2,1,0:T(8,128)(2,1)}, u32[]{:S(2)}) copy-start(bf16[32,96,96]{2,1,0:T(8,128)(2,1)} %rot.1) | copy-start | bytes 1769476
  42.7 6.9 %copy-start.3 = (bf16[16,32,96]{2,1,0:T(8,128)(2,1)S(1)}, bf16[16,32,96]{2,1,0:T(8,128)(2,1)}, u32[]{:S(2)}) copy-start(bf16[16,32,96]{2,1,0:T(8,128)(2,1)} %axial.1) | copy-start | bytes 294916
  42.7 17.0 %all-to-all-start.2 = ((bf16[16,16,384]{2,1,0:T(8,128)(2,1)}), bf16[16,16,384]{2,1,0:T(8,128)(2,1)S(1)}, u32[]{:S(2)}, u32[]{:S(2)}) async-start(bf16[16,16,384]{2,1,0:T(8,128)(2,1)} %couple.1), calls=%async_computation.2 | async-start | bytes 393216 | tf_op jit(solution)/shard_map/all_to_all | solution.py:346
  49.4 0.7 %copy-start.4 = (bf16[96,96]{1,0:T(8,128)(2,1)S(1)}, bf16[96,96]{1,0:T(8,128)(2,1)}, u32[]{:S(2)}) copy-start(bf16[96,96]{1,0:T(8,128)(2,1)} %out_map.1) | copy-start | bytes 55300
  49.4 0.7 %copy-start.5 = (bf16[96,96]{1,0:T(8,128)(2,1)S(1)}, bf16[96,96]{1,0:T(8,128)(2,1)}, u32[]{:S(2)}) copy-start(bf16[96,96]{1,0:T(8,128)(2,1)} %in_map.1) | copy-start | bytes 55300
  49.5 0.7 %copy-start.6 = (f32[16,96]{1,0:T(8,128)S(1)}, f32[16,96]{1,0:T(8,128)}, u32[]{:S(2)}) copy-start(f32[16,96]{1,0:T(8,128)} %tmat.1) | copy-start | bytes 18436
  49.5 0.7 %copy-start.8 = (s32[16]{0:T(128)S(1)}, s32[16]{0:T(128)}, u32[]{:S(2)}) copy-start(s32[16]{0:T(128)} %counts.1) | copy-start | bytes 196
  50.2 1.5 %copy-start.7 = (s32[16,32]{1,0:T(8,128)S(1)}, s32[16,32]{1,0:T(8,128)}, u32[]{:S(2)}) copy-start(s32[16,32]{1,0:T(8,128)} %nbr.1) | copy-start | bytes 6148
